TPU v7x, 256 devices: a whole 4x4x8 slice. The times are simulated.
256 devices in a mesh: seq: 64 (over y, z, core), batch: 4 (over x).
Axes of the slice: x: 4, y: 4, z: 8, core: 2. Of those that a mesh axis runs over, the one named last changes fastest.
Arguments:
- queries: bfloat16 [65536, 256], P(('batch', 'seq')), parts along dimension 0, may hold values from -0.5 to 0.5
- keys: bfloat16 [65536, 256], P(('batch', 'seq')), parts along dimension 0, may hold values from -0.5 to 0.5
- values: bfloat16 [65536, 512], P(('batch', 'seq')), parts along dimension 0, may hold values from -6 to 6
- log_decay: float32 [65536, 256], P(('batch', 'seq')), parts along dimension 0, may hold values from -1 to 0, as said below
- out_grad: bfloat16 [65536, 512], P(('batch', 'seq')), parts along dimension 0, may hold values from -0.19921875 to 0.19921875
Outputs:
- grad_queries: bfloat16 [65536, 256], P(('batch', 'seq')), parts along dimension 0
- grad_keys: bfloat16 [65536, 256], P(('batch', 'seq')), parts along dimension 0
- grad_values: bfloat16 [65536, 512], P(('batch', 'seq')), parts along dimension 0
- grad_decay: float32 [65536, 256], P(('batch', 'seq')), parts along dimension 0
There are 4 independent parts, one for each index of `batch`. A program takes and returns all parts, laid end to end along the dimension named above; each array names one. Nothing has to cross between parts.
Inputs may be any that keep to these rules, and one draw needn't show every extreme that they name: `log_decay`: log of a decay factor per position and key channel.
All inputs are finite; a program needn't handle non-finite values.
Results may differ from a plain program's by a relative error of at most 0.001.
Values sent between devices are 32-bit elements; how exact they have to be, the bound alone decides.
No kernel may reach another device: no remote copies, remote signals or barrier semaphores. Data moves between devices by JAX's collectives and lax.ppermute only.
A program may use at most 128 MiB of HBM per device.

v0:
```python
import jax
import jax.numpy as jnp
from jax import lax
from jax.sharding import Mesh
from jax.sharding import PartitionSpec as P

H = 2
K = 128
V = 256
GROUP = 64
SEQ = ("seq_0", "seq_1", "seq_2")
BATCH_SEQ = ("batch", "seq_0", "seq_1", "seq_2")


HIGHEST_PRECISION = lax.Precision.HIGHEST


def neutral_like(array, identity):
    return jax.tree.map(
        lambda a, e: jnp.broadcast_to(jnp.asarray(e, a.dtype), a.shape), array, identity
    )


def carried_in(array, axes, combine, identity, reverse):
    before = start = neutral_like(array, identity)
    running = array
    for axis in reversed(axes):
        peers, mine = (lax.axis_size(axis), lax.axis_index(axis))
        pieces = jax.tree.map(lambda part: lax.all_gather(part, axis), running)
        inside, running = (start, start)
        for k in reversed(range(peers)) if reverse else range(peers):
            passed = k > mine if reverse else k < mine
            running = combine(running, jax.tree.map(lambda part: part[k], pieces))
            inside = jax.tree.map(lambda new, old: jnp.where(passed, new, old), running, inside)
        before = combine(inside, before)
    return before


def from_everyone(array, axis):
    peers = lax.axis_size(axis)
    return lax.all_to_all(
        jnp.broadcast_to(array[None], (peers, *array.shape)), axis, 0, 0, tiled=True
    )


def combined_pairwise(pieces, combine):
    while len(jax.tree.leaves(pieces)[0]) > 1:
        pieces = jax.vmap(combine)(*(pieces[side::2] for side in (0, 1)))
    return pieces[0]


def prefix_2(array, axis, combine, identity):
    peers, mine = (lax.axis_size(axis), lax.axis_index(axis))
    passed = jnp.arange(peers) > mine

    def kept(part, zero, own):
        part = jnp.where(
            passed.reshape(-1, *(1 for _ in own.shape)), part, jnp.asarray(zero, own.dtype)
        )
        return part[::-1]

    pieces = from_everyone(array, axis)
    return combined_pairwise(kept(pieces, identity, array), combine)


def outer_product(form, left, right):
    return jnp.einsum(
        form, left, right, precision=HIGHEST_PRECISION, preferred_element_type=jnp.float32
    )


def pair_combine(earlier, later_one):
    return (earlier[0] + later_one[0], jnp.exp(later_one[0])[..., None] * earlier[1] + later_one[1])


def add_terms(earlier, later_one):
    return earlier + later_one


def local(queries, keys, values, log_decay, out_grad):
    input_symbols = queries.shape[0]
    blocks = input_symbols // GROUP
    query_rows = queries.reshape(blocks, GROUP, H, K).astype(jnp.float32)
    key_rows = keys.reshape(blocks, GROUP, H, K).astype(jnp.float32)
    value_bf = values.reshape(blocks, GROUP, H, V)
    grad_bf = out_grad.reshape(blocks, GROUP, H, V)
    value_rows = value_bf.astype(jnp.float32)
    grad_rows = grad_bf.astype(jnp.float32)
    within = jnp.cumsum(log_decay.reshape(blocks, GROUP, H, K), axis=1)
    block_sum = within[:, -1]
    rising = jnp.exp(within)
    falling = jnp.exp(-within)
    tail_gate = jnp.exp(block_sum[:, None] - within)
    q_gate = query_rows * rising
    k_gate = key_rows * falling
    k_tail = key_rows * tail_gate
    local_ends = outer_product("nchk,nchv->nhkv", k_tail, value_rows)
    local_starts = outer_product("nchk,nchv->nhkv", q_gate, grad_rows)
    zero_state = jnp.zeros((H, K, V), jnp.float32)
    zero_decay = jnp.zeros((H, K), jnp.float32)

    def forward_step(carried_state, inputs):
        summed_decay, end_state = inputs
        return (jnp.exp(summed_decay)[..., None] * carried_state + end_state, carried_state)

    device_end, prefix = lax.scan(forward_step, zero_state, (block_sum, local_ends))

    def backward_step(carried_gradient, inputs):
        summed_decay, start_grad = inputs
        return (start_grad + jnp.exp(summed_decay)[..., None] * carried_gradient, carried_gradient)

    device_start, suffix = lax.scan(
        backward_step, zero_state, (block_sum, local_starts), reverse=True
    )
    device_total = jnp.sum(block_sum, axis=0)
    through = lax.cumsum(block_sum, axis=0)
    prior_decay = through - block_sum
    after_decay = device_total[None] - through
    entry_pair = carried_in(
        (device_total, device_end), SEQ, pair_combine, (zero_decay, zero_state), False
    )
    starts = prefix + jnp.exp(prior_decay)[..., None] * entry_pair[1]
    causal = jnp.tril(jnp.ones((GROUP, GROUP), jnp.float32))
    score_matrix = outer_product("nthk,nshk->nhts", q_gate, k_gate) * causal
    pair_dots = (
        jnp.einsum("nthv,nshv->nhts", grad_bf, value_bf, preferred_element_type=jnp.float32)
        * causal
    )
    grad_q = rising * (
        outer_product("nhts,nshk->nthk", pair_dots, k_gate)
        + outer_product("nthv,nhkv->nthk", grad_rows, starts)
    )
    inner_k = falling * outer_product("nhts,nthk->nshk", pair_dots, q_gate)
    exit_pair = carried_in(
        (device_total, device_start), SEQ, pair_combine, (zero_decay, zero_state), True
    )
    exit_grad = exit_pair[1]
    grads_in = suffix + jnp.exp(after_decay)[..., None] * exit_grad
    grad_k = inner_k + tail_gate * outer_product("nshv,nhkv->nshk", value_rows, grads_in)
    value_gradient = outer_product("nhts,nthv->nshv", score_matrix, grad_rows) + outer_product(
        "nshk,nhkv->nshv", k_tail, grads_in
    )
    dg_terms = (query_rows * grad_q - key_rows * grad_k).reshape(input_symbols, H * K)
    running = lax.cumsum(dg_terms, axis=0, reverse=True)
    later_sum = prefix_2(running[0], SEQ, add_terms, jnp.zeros((H * K,), jnp.float32))
    grad_decay = running + later_sum[None, :]
    return (
        grad_q.reshape(input_symbols, H * K).astype(jnp.bfloat16),
        grad_k.reshape(input_symbols, H * K).astype(jnp.bfloat16),
        value_gradient.reshape(input_symbols, H * V).astype(jnp.bfloat16),
        grad_decay,
    )


def solution(mesh):
    finer = Mesh(
        mesh.devices.reshape(4, 8, 2, mesh.shape["batch"]), ("seq_0", "seq_1", "seq_2", "batch")
    )
    in_specs = (
        P(BATCH_SEQ, None),
        P(BATCH_SEQ, None),
        P(BATCH_SEQ, None),
        P(BATCH_SEQ, None),
        P(BATCH_SEQ, None),
    )
    out_specs = (P(BATCH_SEQ, None), P(BATCH_SEQ, None), P(BATCH_SEQ, None), P(BATCH_SEQ, None))
    return jax.shard_map(local, mesh=finer, in_specs=in_specs, out_specs=out_specs, check_vma=False)
```

profile of v0, /device:TPU:1, one launch (start us, length us, event | category | flops | bytes accessed | tf_op | source)
XLA Modules:
  0.0 199.8 jit_solution(2636079725747692072)
XLA Ops:
  7.2 1.1 reshape.354
  8.4 1.0 reshape.356
  9.5 1.0 reshape.360
  11.1 1.1 broadcast.255.clone
  12.2 3.5 %while.30 = (s32[]{:T(128)}, f32[2,128,256]{2,1,0:T(8,128)S(1)}, f32[4,2,128,256]{3,2,1,0:T(8,128)}, f32[4,2,128]{2,1,0:T(2,128)S(1)}, f32[4,2,128,256]{3,2,1,0:T(8,128)S(1)}, /*index=5*/s32[]{:T(128)}, s32[]{:T(128)}) while((s32[]{:T(128)}, f32[2,128,256]{2,1,0:T(8,128)S(1)}, f32[4,2,128,256]{3,2,1,0:T(8,128)}, ...), condition=%wide.region_2.3_spmd.clone, body=%wide.region_1.2_spmd.clone.sunk | while | flops 262147 | bytes 1313900 | solution.py:106
  15.8 5.1 %all-gather.1 = f32[4,128,256]{2,1,0:T(8,128)S(1)} all-gather(f32[2,128,256]{2,1,0:T(8,128)S(1)} %get-tuple-element.137), channel_id=3, replica_groups=mesh['seq_0'=4,'seq_1'=8,'seq_2'=2,'batch'=4] {'seq_2'}, dimensions={0}, use_global_device_ids=true | all-gather | bytes 786432 | tf_op jit(solution)/shard_map/all_gather | solution.py:29
  20.9 1.8 all-gather.4
  26.2 2.2 %all-gather.2 = f32[4,128,256]{2,1,0:T(8,128)S(1)} all-gather(f32[2,128,256]{2,1,0:T(8,128)S(1)} %get-tuple-element.139), channel_id=4, replica_groups=mesh['seq_0'=4,'seq_1'=8,'seq_2'=2,'batch'=4] {'seq_2'}, dimensions={0}, use_global_device_ids=true | all-gather | bytes 786432 | tf_op jit(solution)/shard_map/all_gather | solution.py:29
  29.3 14.0 %all-gather.5 = f32[8,2,128]{2,1,0:T(2,128)S(1)} all-gather(f32[1,2,128]{2,1,0:T(2,128)S(1)} %get-tuple-element.197), channel_id=5, replica_groups=mesh['seq_0'=4,'seq_1'=8,'seq_2'=2,'batch'=4] {'seq_1'}, dimensions={0}, use_global_device_ids=true | all-gather | bytes 9216 | tf_op jit(solution)/shard_map/all_gather | solution.py:29
  43.3 18.0 %all-gather.11.cloned.1.call-done = f32[8,2,128,256]{3,2,1,0:T(8,128)} async-done(((f32[1,2,128,256]{3,2,1,0:T(8,128)}), f32[8,2,128,256]{3,2,1,0:T(8,128)}) %all-gather.11.cloned.1.call-update) | async-done | bytes 2097168 | tf_op jit(solution)/shard_map/all_gather | solution.py:29
  61.3 2.6 %slice_add_fusion.16 = (f32[1,2,128,256]{3,2,1,0:T(8,128)}, f32[1,2,128,256]{3,2,1,0:T(8,128)}) fusion(f32[8,2,128,256]{3,2,1,0:T(8,128)} %all-gather.11.cloned.1.call-done, f32[2,128]{1,0:T(2,128)S(1)} %get-tuple-element.212, f32[2,128]{1,0:T(2,128)S(1)} %get-tuple-element.211, f32[2,128]{1,0:T(2,128)S(1)} %get-tuple-element.214, ...), kind=kLoop, calls=%fused_computation.59 | loop fusion | flops 983040 | bytes 2629632 | tf_op jit(solution)/shard_map/add | solution.py:73
  64.0 7.7 %all_gather.53 = f32[4,2,128]{2,1,0:T(2,128)S(1)} all-gather(f32[1,2,128]{2,1,0:T(2,128)S(1)} %get-tuple-element.208), channel_id=1, replica_groups=mesh['seq_0'=4,'seq_1'=8,'seq_2'=2,'batch'=4] {'seq_0'}, dimensions={0}, use_global_device_ids=true | all-gather | bytes 5120 | tf_op jit(solution)/shard_map/all_gather | solution.py:29
  71.7 5.7 %all_gather.58 = f32[4,2,128]{2,1,0:T(2,128)S(1)} all-gather(f32[1,2,128]{2,1,0:T(2,128)S(1)} %get-tuple-element.207), channel_id=1, replica_groups=mesh['seq_0'=4,'seq_1'=8,'seq_2'=2,'batch'=4] {'seq_0'}, dimensions={0}, use_global_device_ids=true | all-gather | bytes 5120 | tf_op jit(solution)/shard_map/all_gather | solution.py:29
  77.5 25.1 %all-gather.15.cloned.1.call-done = f32[8,2,128,256]{3,2,1,0:T(8,128)} async-done(((f32[1,2,128,256]{3,2,1,0:T(8,128)}), f32[8,2,128,256]{3,2,1,0:T(8,128)}) %all-gather.15.cloned.1.call-update) | async-done | bytes 2097168 | tf_op jit(solution)/shard_map/all_gather | solution.py:29
  102.6 2.7 %slice_add_fusion.4 = (f32[1,2,128,256]{3,2,1,0:T(8,128)}, f32[1,2,128,256]{3,2,1,0:T(8,128)}) fusion(f32[8,2,128,256]{3,2,1,0:T(8,128)} %all-gather.15.cloned.1.call-done, f32[2,128]{1,0:T(2,128)S(1)} %get-tuple-element.218, f32[2,128]{1,0:T(2,128)S(1)} %get-tuple-element.217, f32[2,128]{1,0:T(2,128)S(1)} %get-tuple-element.215, ...), kind=kLoop, calls=%fused_computation.39 | loop fusion | flops 983040 | bytes 2629632 | tf_op jit(solution)/shard_map/add | solution.py:73
  105.3 0.9 convolution_multiply_fusion.1
  106.9 1.3 convolution_bitcast_fusion.1
  108.1 24.3 %all-gather.13.cloned.1.call-done = f32[4,2,128,256]{3,2,1,0:T(8,128)} async-done(((f32[1,2,128,256]{3,2,1,0:T(8,128)}), f32[4,2,128,256]{3,2,1,0:T(8,128)}) %all-gather.13.cloned.1.call-update) | async-done | bytes 1048592 | tf_op jit(solution)/shard_map/all_gather | solution.py:29
  132.4 2.3 %fusion.25 = f32[2,128,256]{2,1,0:T(8,128)S(1)} fusion(f32[4,2,128,256]{3,2,1,0:T(8,128)} %all-gather.13.cloned.1.call-done, f32[1,2,128,256]{3,2,1,0:T(8,128)} %get-tuple-element.200, f32[1,2,128,256]{3,2,1,0:T(8,128)} %get-tuple-element.201, f32[8,2,128,256]{3,2,1,0:T(8,128)} %all-gather.11.cloned.1.call-done, f32[4,128,256]{2,1,0:T(8,128)S(1)} %copy-done.1, ...), kind=kLoop, calls=%fused_computation.55 | loop fusion | flops 2555904 | bytes 3946510 | tf_op jit(solution)/shard_map/mul | solution.py:122
  136.0 25.1 %all-gather.17.cloned.1.call-done = f32[4,2,128,256]{3,2,1,0:T(8,128)} async-done(((f32[1,2,128,256]{3,2,1,0:T(8,128)}), f32[4,2,128,256]{3,2,1,0:T(8,128)}) %all-gather.17.cloned.1.call-update) | async-done | bytes 1048592 | tf_op jit(solution)/shard_map/all_gather | solution.py:29
  161.1 2.2 %fusion.19 = f32[2,128,256]{2,1,0:T(8,128)S(1)} fusion(f32[4,2,128,256]{3,2,1,0:T(8,128)} %all-gather.17.cloned.1.call-done, f32[1,2,128,256]{3,2,1,0:T(8,128)S(1)} %copy-done.5, f32[1,2,128,256]{3,2,1,0:T(8,128)} %get-tuple-element.199, f32[8,2,128,256]{3,2,1,0:T(8,128)} %all-gather.15.cloned.1.call-done, f32[4,128,256]{2,1,0:T(8,128)S(1)} %all-gather.2, ...), kind=kLoop, calls=%fused_computation.35 | loop fusion | flops 2555904 | bytes 3946510 | tf_op jit(solution)/shard_map/mul | solution.py:138
  167.4 2.3 %fusion.28 = f32[256,2,128]{0,1,2:T(2,128)S(1)} fusion(f32[256,2,128]{0,2,1:T(8,128)S(1)} %bitcast.267), kind=kOutput, calls=%fused_computation.71 | output fusion | flops 8323072 | bytes 524288 | tf_op jit(solution)/shard_map/reduce-window
  170.5 11.8 %all-to-all-start = ((f32[64,1,256]{2,1,0:T(1,128)}), f32[64,1,256]{2,1,0:T(1,128)S(1)}, u32[]{:S(2)}, u32[]{:S(2)}) async-start(f32[64,1,256]{2,1,0:T(1,128)} %broadcast_in_dim.46), calls=%async_computation | async-start | bytes 131072 | tf_op jit(solution)/shard_map/all_to_all | solution.py:41
  183.0 9.0 %all-to-all-done = f32[64,1,256]{2,1,0:T(1,128)S(1)} async-done(((f32[64,1,256]{2,1,0:T(1,128)}), f32[64,1,256]{2,1,0:T(1,128)S(1)}, u32[]{:S(2)}, u32[]{:S(2)}) %all-to-all-start) | async-done | bytes 65568 | tf_op jit(solution)/shard_map/all_to_all | solution.py:41
  (119 shorter events, 17.8 us)
Async XLA Ops:
  7.2 54.1 %all-gather.11.cloned.1.call-start = ((), (), s32[]{:S(2)}) async-start(), calls=%async_computation.1 | async-start | bytes 2359296 | tf_op jit(solution)/shard_map/all_gather | solution.py:29
  12.2 11.5 %copy-start.9 = (bf16[256,512]{1,0:T(8,128)(2,1)S(1)}, bf16[256,512]{1,0:T(8,128)(2,1)}, u32[]{:S(2)}) copy-start(bf16[256,512]{1,0:T(8,128)(2,1)} %param.13) | copy-start | bytes 786436
  15.7 8.0 %copy-start.10 = (bf16[256,256]{1,0:T(8,128)(2,1)S(1)}, bf16[256,256]{1,0:T(8,128)(2,1)}, u32[]{:S(2)}) copy-start(bf16[256,256]{1,0:T(8,128)(2,1)} %param.9) | copy-start | bytes 393220
  20.9 3.0 %copy-start = (f32[4,128,256]{2,1,0:T(8,128)}, f32[4,128,256]{2,1,0:T(8,128)S(1)}, u32[]{:S(2)}) copy-start(f32[4,128,256]{2,1,0:T(8,128)S(1)} %all-gather.1) | copy-start | bytes 1572868
  23.6 79.0 %all-gather.15.cloned.1.call-start = ((), (), s32[]{:S(2)}) async-start(), calls=%async_computation.3 | async-start | bytes 2359296 | tf_op jit(solution)/shard_map/all_gather | solution.py:29
  23.9 0.7 copy-start.3
  29.3 103.1 %all-gather.13.cloned.1.call-start = ((), (), s32[]{:S(2)}) async-start(), calls=%async_computation.2 | async-start | bytes 1310720 | tf_op jit(solution)/shard_map/all_gather | solution.py:29
  63.9 42.4 %copy-start.4 = (f32[4,64,2,128]{3,2,1,0:T(2,128)S(1)}, f32[4,64,2,128]{3,2,1,0:T(2,128)}, u32[]{:S(2)}) copy-start(f32[4,64,2,128]{3,2,1,0:T(2,128)} %copy-done.3) | copy-start | bytes 786436
  63.9 97.2 %all-gather.17.cloned.1.call-start = ((), (), s32[]{:S(2)}) async-start(), calls=%async_computation.4 | async-start | bytes 1310720 | tf_op jit(solution)/shard_map/all_gather | solution.py:29
  105.3 27.1 %copy-start.1 = (f32[4,128,256]{2,1,0:T(8,128)S(1)}, f32[4,128,256]{2,1,0:T(8,128)}, u32[]{:S(2)}) copy-start(f32[4,128,256]{2,1,0:T(8,128)} %copy-done) | copy-start | bytes 1572868
  132.4 2.3 %copy-start.2 = (f32[4,2,128,256]{3,2,1,0:T(8,128)S(1)}, f32[4,2,128,256]{3,2,1,0:T(8,128)}, u32[]{:S(2)}) copy-start(f32[4,2,128,256]{3,2,1,0:T(8,128)} %get-tuple-element.136) | copy-start | bytes 3145732
  132.4 3.2 %copy-start.6 = (f32[4,2,64,64]{3,2,1,0:T(8,128)S(1)}, f32[4,2,64,64]{3,2,1,0:T(8,128)}, u32[]{:S(2)}) copy-start(f32[4,2,64,64]{3,2,1,0:T(8,128)} %convolution_multiply_fusion.1) | copy-start | bytes 393220
  134.7 26.4 %copy-start.5 = (f32[1,2,128,256]{3,2,1,0:T(8,128)S(1)}, f32[1,2,128,256]{3,2,1,0:T(8,128)}, u32[]{:S(2)}) copy-start(f32[1,2,128,256]{3,2,1,0:T(8,128)} %get-tuple-element.198) | copy-start | bytes 786436
  161.1 3.2 %copy-start.7 = (f32[4,2,64,64]{3,2,1,0:T(8,128)S(1)}, f32[4,2,64,64]{3,2,1,0:T(8,128)}, u32[]{:S(2)}) copy-start(f32[4,2,64,64]{3,2,1,0:T(8,128)} %convolution_multiply_fusion.1) | copy-start | bytes 393220
  163.4 1.8 copy-start.8
  170.5 21.6 %all-to-all-start = ((f32[64,1,256]{2,1,0:T(1,128)}), f32[64,1,256]{2,1,0:T(1,128)S(1)}, u32[]{:S(2)}, u32[]{:S(2)}) async-start(f32[64,1,256]{2,1,0:T(1,128)} %broadcast_in_dim.46), calls=%async_computation | async-start | bytes 131072 | tf_op jit(solution)/shard_map/all_to_all | solution.py:41
Sparse Core Ops, SparseCore 0:
  23.7 37.5 all-gather.10
  63.1 39.4 all-gather.14
  105.0 27.3 all-gather.12
  134.1 27.0 all-gather.16
where the time goes:
time: 200 us
  waiting for transfers between devices  102 us (51%)
  blocking collectives  36.4 us (18%)
  other arithmetic  18.9 us (9%)
  between operations  14.2 us (7%)
  starting transfers between devices  12 us (6%)
  local copies, waits for them, and re-layouts  8.58 us (4%)
  matrix products  7.78 us (4%)
    all_gather x4, waiting for transfers between devices, carried_in(): pieces = jax.tree.map(lambda part: lax.all_gather(part, axis), running)  92.5 us
    all_gather x6, blocking collectives, carried_in(): pieces = jax.tree.map(lambda part: lax.all_gather(part, axis), running)  36.4 us
    all_to_all x1, starting transfers between devices, from_everyone(): lax.all_to_all(jnp.broadcast_to(array[None], (peers, *array.shape)), axis...  11.8 us
    all_to_all x1, waiting for transfers between devices, from_everyone(): lax.all_to_all(jnp.broadcast_to(array[None], (peers, *array.shape)), axis...  9.04 us
    add x4, other arithmetic, pair_combine(): jnp.exp(later_one[0])[..., None] * earlier[1] + later_one[1]  6.96 us
    dot_general x9, matrix products, outer_product(): jnp.einsum(form, left, right, precision=HIGHEST_PRECISION, preferred_elem...  6.85 us
  transfers between devices with their start and end apart: 5, of which 5 were waited for; matrix products, arithmetic and copies ran while one was open for 7% of the time, Pallas kernels for 0%

commit v1 on v0

v1 whole, which is shorter than its diff:
```python
import jax
import jax.numpy as jnp
from jax import lax
from jax.experimental import pallas as pl
from jax.experimental.pallas import tpu as pltpu
from jax.sharding import Mesh
from jax.sharding import PartitionSpec as P

H = 2
K = 128
V = 256
GROUP = 64
TOK = 256
HK = H * K
Y, Z, CORES = 4, 8, 2
CHIPS = Y * Z
ROWS = V // CHIPS
MSG = ROWS + 1
CHIP_AXES = ("seq_y", "seq_z")
SPEC = P(("batch", "seq_y", "seq_z", "seq_c"), None)
F32 = jnp.float32
BF16 = jnp.bfloat16


def dot(left, right, dims):
    return lax.dot_general(left, right, (dims, ((), ())), preferred_element_type=F32)


def nn(left, right):
    return dot(left, right, ((1,), (0,)))


def nt(left, right):
    return dot(left, right, ((1,), (1,)))


def tn(left, right):
    return dot(left, right, ((0,), (0,)))


def split(x):
    hi = x.astype(BF16)
    return hi, (x - hi.astype(F32)).astype(BF16)


def split3(x):
    hi = x.astype(BF16)
    rest = x - hi.astype(F32)
    mid = rest.astype(BF16)
    return hi, mid, (rest - mid.astype(F32)).astype(BF16)


def summed(x, suffix):
    rows = x.shape[0]
    r = lax.broadcasted_iota(jnp.int32, (rows, rows), 0)
    c = lax.broadcasted_iota(jnp.int32, (rows, rows), 1)
    ones = jnp.where((c >= r) if suffix else (c <= r), 1.0, 0.0).astype(BF16)
    hi, mid, lo = split3(x)
    return nn(ones, hi) + (nn(ones, mid) + nn(ones, lo))


def head(h, width):
    return slice(h * width, (h + 1) * width)


def folded(out):
    half = out.shape[1] // 2
    return out[:, :half] + out[:, half:]


def ends_kernel(q_ref, k_ref, v_ref, do_ref, g_ref, send_ref, e_ref, f_ref, b_ref):
    first = lax.axis_index("seq_c") == 0
    b = summed(g_ref[...], False)
    b_ref[...] = b
    total = b[TOK - 1 :]
    k_tail = k_ref[...].astype(F32) * jnp.exp(total - b)
    q_gate = q_ref[...].astype(F32) * jnp.exp(b)
    for h in range(H):
        hk, hv = head(h, K), head(h, V)
        e_ref[:, hk] = folded(tn(v_ref[:, hv], jnp.concatenate(split(k_tail[:, hk]), 1)))
        f_ref[:, hk] = folded(tn(do_ref[:, hv], jnp.concatenate(split(q_gate[:, hk]), 1)))

    @pl.when(first)
    def _():
        send_ref[:V] = f_ref[...]

    @pl.when(jnp.logical_not(first))
    def _():
        send_ref[:V] = e_ref[...]

    send_ref[V:] = jnp.broadcast_to(total, (8, HK))


def message_kernel(e_ref, f_ref, b_ref, got_ref, msg_ref):
    first = lax.axis_index("seq_c") == 0
    total = b_ref[TOK - 1 :]
    other = got_ref[V : V + 1]
    gate = jnp.exp(other)
    chip_gate = jnp.exp(total + other)

    def write(kept_ref):
        for i in range(CHIPS):
            rows = slice(i * ROWS, (i + 1) * ROWS)
            msg_ref[i * MSG : i * MSG + ROWS, 0, :] = kept_ref[rows] * gate + got_ref[rows]
            msg_ref[i * MSG + ROWS] = chip_gate

    @pl.when(first)
    def _():
        write(e_ref)

    @pl.when(jnp.logical_not(first))
    def _():
        write(f_ref)


def scan_kernel(msg_ref, out_ref):
    first = lax.axis_index("seq_c") == 0
    state = jnp.zeros((ROWS, HK), F32)
    for i in range(CHIPS):
        at = jnp.where(first, i, CHIPS - 1 - i)
        out_ref[pl.ds(pl.multiple_of(at * ROWS, ROWS), ROWS)] = state
        state = msg_ref[at * MSG + ROWS] * state + msg_ref[pl.ds(at * MSG, ROWS), 0, :]


def onward_kernel(e_ref, f_ref, b_ref, came_ref, send_ref):
    first = lax.axis_index("seq_c") == 0
    gate = jnp.exp(b_ref[TOK - 1 :])

    @pl.when(first)
    def _():
        send_ref[...] = gate * came_ref[...] + e_ref[...]

    @pl.when(jnp.logical_not(first))
    def _():
        send_ref[...] = gate * came_ref[...] + f_ref[...]


def inner_kernel(q_ref, k_ref, v_ref, do_ref, b_ref, dq_ref, dk_ref, dv_ref):
    r = lax.broadcasted_iota(jnp.int32, (TOK, TOK), 0)
    c = lax.broadcasted_iota(jnp.int32, (TOK, TOK), 1)
    for h in range(H):
        hk, hv = head(h, K), head(h, V)
        q = q_ref[:, hk].astype(F32)
        k = k_ref[:, hk].astype(F32)
        b = b_ref[:, hk]
        pair = jnp.where(c <= r, nt(do_ref[:, hv], v_ref[:, hv]), 0.0)
        pair_t = jnp.where(c >= r, nt(v_ref[:, hv], do_ref[:, hv]), 0.0)
        p_hi, p_lo = split(pair)
        t_hi, t_lo = split(pair_t)
        dk = jnp.zeros((TOK, K), F32)
        dv = jnp.zeros((TOK, V), F32)
        for i in range(TOK // GROUP):
            rows = slice(i * GROUP, (i + 1) * GROUP)
            end = (i + 1) * GROUP
            upto = slice(0, end)
            start = b[i * GROUP - 1 : i * GROUP] if i else jnp.zeros((1, K), F32)
            rising = jnp.exp(b[rows] - start)
            falling = jnp.exp(start - b[upto])
            q_hi, q_lo = split(q[rows] * rising)
            k_hi, k_lo = split(k[upto] * falling)
            scores_t = nt(k_hi, q_hi) + (nt(k_hi, q_lo) + nt(k_lo, q_hi))
            rr = lax.broadcasted_iota(jnp.int32, (end, GROUP), 0)
            cc = lax.broadcasted_iota(jnp.int32, (end, GROUP), 1) + i * GROUP
            s_hi, s_lo = split(jnp.where(cc >= rr, scores_t, 0.0))
            k_both = jnp.concatenate((k_hi, k_lo), 1)
            q_both = jnp.concatenate((q_hi, q_lo), 1)
            dq_ref[rows, hk] = rising * (
                folded(nn(p_hi[rows, upto], k_both)) + nn(p_lo[rows, upto], k_hi)
            )
            dk_part = falling * (folded(nn(t_hi[upto, rows], q_both)) + nn(t_lo[upto, rows], q_hi))
            dv_part = nn(s_hi, do_ref[rows, hv]) + nn(s_lo, do_ref[rows, hv])
            if end < TOK:
                dk_part = jnp.concatenate((dk_part, jnp.zeros((TOK - end, K), F32)), 0)
                dv_part = jnp.concatenate((dv_part, jnp.zeros((TOK - end, V), F32)), 0)
            dk = dk + dk_part
            dv = dv + dv_part
        dk_ref[:, hk] = dk
        dv_ref[:, hv] = dv


def grads_kernel(
    q_ref, k_ref, v_ref, do_ref, b_ref, e_ref, came_ref, got_ref, dqi_ref, dki_ref, dvi_ref,
    dq_ref, dk_ref, dv_ref, dg_ref, s_ref, g_ref,
):
    first = lax.axis_index("seq_c") == 0

    @pl.when(first)
    def _():
        s_ref[...] = came_ref[...]
        g_ref[...] = got_ref[...]

    @pl.when(jnp.logical_not(first))
    def _():
        s_ref[...] = got_ref[...]
        g_ref[...] = came_ref[...]

    for h in range(H):
        hk, hv = head(h, K), head(h, V)
        q = q_ref[:, hk].astype(F32)
        k = k_ref[:, hk].astype(F32)
        b = b_ref[:, hk]
        total = b[TOK - 1 :]
        rising = jnp.exp(b)
        tail = jnp.exp(total - b)
        state = s_ref[:, hk]
        grad = g_ref[:, hk]
        g_hi, g_lo = split(grad)
        dq = dqi_ref[:, hk] + rising * folded(
            nn(do_ref[:, hv], jnp.concatenate(split(state), 1))
        )
        dk = dki_ref[:, hk] + tail * folded(
            nn(v_ref[:, hv], jnp.concatenate((g_hi, g_lo), 1))
        )
        t_hi, t_lo = split(k * tail)
        dv = dvi_ref[:, hv] + (nt(t_hi, g_hi) + (nt(t_lo, g_hi) + nt(t_hi, g_lo)))
        dq_ref[:, hk] = dq.astype(BF16)
        dk_ref[:, hk] = dk.astype(BF16)
        dv_ref[:, hv] = dv.astype(BF16)
        end_state = jnp.exp(total) * state + e_ref[:, hk]
        later = jnp.sum(end_state * grad, axis=0, keepdims=True)
        dg_ref[:, hk] = summed(q * dq - k * dk, True) + later


def call(kernel, outs, *args, scratch=(), flops=1000000):
    whole = pl.BlockSpec(memory_space=pltpu.VMEM)
    shapes = [jax.ShapeDtypeStruct(shape, dtype) for shape, dtype in outs]
    out = pl.pallas_call(
        kernel,
        out_shape=shapes,
        in_specs=[whole] * len(args),
        out_specs=[whole] * len(outs),
        scratch_shapes=list(scratch),
        cost_estimate=pl.CostEstimate(flops=flops, bytes_accessed=2000000, transcendentals=0),
        compiler_params=pltpu.CompilerParams(vmem_limit_bytes=32 << 20),
    )(*args)
    return out if len(outs) > 1 else out[0]


SWAP = [(0, 1), (1, 0)]
SQUARE = ((TOK, HK), F32)


def local(q, k, v, log_decay, do):
    send, e, f, b = call(
        ends_kernel, [((V + 8, HK), F32), SQUARE, SQUARE, SQUARE], q, k, v, do, log_decay
    )
    got = lax.ppermute(send, "seq_c", SWAP)
    msg = call(message_kernel, [((CHIPS * MSG, 1, HK), F32)], e, f, b, got)
    msg = lax.all_to_all(msg, CHIP_AXES, 0, 0, tiled=True)
    back = call(scan_kernel, [SQUARE], msg)
    came = lax.all_to_all(
        back.reshape(CHIPS, ROWS, HK), CHIP_AXES, 0, 0, tiled=True
    ).reshape(V, HK)
    onward = call(onward_kernel, [SQUARE], e, f, b, came)
    got = lax.ppermute(onward, "seq_c", SWAP)
    inner = call(
        inner_kernel, [SQUARE, SQUARE, ((TOK, H * V), F32)], q, k, v, do, b, flops=200000000
    )
    return call(
        grads_kernel,
        [((TOK, HK), BF16), ((TOK, HK), BF16), ((TOK, H * V), BF16), SQUARE],
        q, k, v, do, b, e, came, got, *inner,
        scratch=[pltpu.VMEM((V, HK), F32)] * 2,
    )


def solution(mesh):
    finer = Mesh(
        mesh.devices.reshape(Y, Z, CORES, mesh.shape["batch"]),
        ("seq_y", "seq_z", "seq_c", "batch"),
    )
    return jax.shard_map(
        local, mesh=finer, in_specs=(SPEC,) * 5, out_specs=(SPEC,) * 4, check_vma=False
    )
```

time: 200 us -> 54.3 us (0.27)
  waiting for transfers between devices: 102 us -> 1.18 us
  other arithmetic: 18.9 us -> 0 us
  between operations: 14.2 us -> 0.69 us
  matrix products: 7.78 us -> 0 us
  starting transfers between devices: 12 us -> 7.02 us
  Pallas kernels: 0 us -> 4.45 us
  local copies, waits for them, and re-layouts: 8.58 us -> 4.67 us
    all_gather x4 -> x0, waiting for transfers between devices: 92.5 us -> none  [carried_in(): pieces = jax.tree.map(lambda part: lax.all_gather(part, axis), running)]
    all_gather x6 -> x0, blocking collectives: 36.4 us -> none  [carried_in(): pieces = jax.tree.map(lambda part: lax.all_gather(part, axis), running)]
    all_to_all x0 -> x2, blocking collectives: none -> 36 us  [the longest x1 19.5 us: local(): msg = lax.all_to_all(msg, CHIP_AXES, 0, 0, tiled=True)]
    all_to_all x1 -> x0, starting transfers between devices: 11.8 us -> none  [from_everyone(): lax.all_to_all(jnp.broadcast_to(array[None], (peers, *array.shape)), axis...]
    all_to_all x1 -> x0, waiting for transfers between devices: 9.04 us -> none  [from_everyone(): lax.all_to_all(jnp.broadcast_to(array[None], (peers, *array.shape)), axis...]
    add x20 -> x0, other arithmetic: 8.74 us -> none  [the longest x4 6.96 us: pair_combine(): jnp.exp(later_one[0])[..., None] * earlier[1] + later_one[1]]
    dot_general x10 -> x0, matrix products: 7.78 us -> none  [the longest x9 6.85 us: outer_product(): jnp.einsum(form, left, right, precision=HIGHEST_PRECISION, preferred_elem...]
    ppermute x0 -> x2, starting transfers between devices: none -> 7.02 us  [the longest x1 3.75 us: local(): got = lax.ppermute(onward, 'seq_c', SWAP)]
  transfers between devices with their start and end apart: 5 -> 2, of which waited for: 5 -> 1; matrix products, arithmetic and copies ran while one was open for 7% -> 0% of each run, Pallas kernels for 0% -> 3%
where the time goes in v1:
time: 54.3 us; the launch traced here: 54 us
  blocking collectives  36 us (66%)
  starting transfers between devices  7.02 us (13%)
  local copies, waits for them, and re-layouts  4.67 us (9%)
  Pallas kernels  4.45 us (8%)
  waiting for transfers between devices  1.18 us (2%)
  between operations  0.69 us (1%)
    all_to_all x1, blocking collectives, local(): msg = lax.all_to_all(msg, CHIP_AXES, 0, 0, tiled=True)  19.5 us
    all_to_all x1, blocking collectives, local(): lax.all_to_all(back.reshape(CHIPS, ROWS, HK), CHIP_AXES, 0, 0, tiled=True)  16.5 us
    unnamed x18, local copies, waits for them, and re-layouts  4.67 us
    pallas_call x6, Pallas kernels, call(): pl.pallas_call(kernel, out_shape=shapes, in_specs=[whole] * len(args), ou...  4.45 us
    ppermute x1, starting transfers between devices, local(): got = lax.ppermute(onward, 'seq_c', SWAP)  3.75 us
    ppermute x1, starting transfers between devices, local(): got = lax.ppermute(send, 'seq_c', SWAP)  3.28 us
    ppermute x1, waiting for transfers between devices, local(): got = lax.ppermute(send, 'seq_c', SWAP)  1.17 us
  transfers between devices with their start and end apart: 2, of which 1 were waited for; matrix products, arithmetic and copies ran while one was open for 0% of the time, Pallas kernels for 3%

profile of v1, /device:TPU:1, one launch (start us, length us, event | category | flops | bytes accessed | tf_op | source)
XLA Modules:
  0.0 54.0 jit_solution(15438178408581835277)
XLA Ops:
  0.6 0.0 copy-start
  0.6 0.9 %copy-done = bf16[256,512]{1,0:T(8,128)(2,1)S(1)} copy-done((bf16[256,512]{1,0:T(8,128)(2,1)S(1)}, bf16[256,512]{1,0:T(8,128)(2,1)}, u32[]{:S(2)}) %copy-start) | copy-done | bytes 262168
  1.6 0.0 copy-start.2
  1.6 0.9 %copy-done.2 = bf16[256,512]{1,0:T(8,128)(2,1)S(1)} copy-done((bf16[256,512]{1,0:T(8,128)(2,1)S(1)}, bf16[256,512]{1,0:T(8,128)(2,1)}, u32[]{:S(2)}) %copy-start.2) | copy-done | bytes 262168
  2.5 0.0 copy-start.4
  2.5 0.9 %copy-done.4 = bf16[256,256]{1,0:T(8,128)(2,1)S(1)} copy-done((bf16[256,256]{1,0:T(8,128)(2,1)S(1)}, bf16[256,256]{1,0:T(8,128)(2,1)}, u32[]{:S(2)}) %copy-start.4) | copy-done | bytes 131096
  3.4 0.9 %copy-done.6 = bf16[256,256]{1,0:T(8,128)(2,1)S(1)} copy-done((bf16[256,256]{1,0:T(8,128)(2,1)S(1)}, bf16[256,256]{1,0:T(8,128)(2,1)}, u32[]{:S(2)}) %copy-start.6) | copy-done | bytes 131096
  4.3 0.9 %copy-done.8 = f32[256,256]{1,0:T(8,128)S(1)} copy-done((f32[256,256]{1,0:T(8,128)S(1)}, f32[256,256]{1,0:T(8,128)}, u32[]{:S(2)}) %copy-start.8) | copy-done | bytes 262168
  5.3 0.8 %shard_map.84 = (f32[264,256]{1,0:T(8,128)S(1)}, f32[256,256]{1,0:T(8,128)S(1)}, f32[256,256]{1,0:T(8,128)S(1)}, f32[256,256]{1,0:T(8,128)S(1)}) custom-call(bf16[256,256]{1,0:T(8,128)(2,1)S(1)} %copy-done.4, bf16[256,256]{1,0:T(8,128)(2,1)S(1)} %copy-done.6, bf16[256,512]{1,0:T(8,128)(2,1)S(1)} %copy-done, bf16[256,512]{1,0:T(8,128)(2,1)S(1)} %copy-done.2, ...), custom_call_target="tpu_custom_call" | custom-call | flops 1000000 | bytes 2000000 | tf_op jit(solution)/shard_map/pallas_call | solution.py:227
  6.1 3.3 %collective-permute-start = (f32[264,256]{1,0:T(8,128)S(1)}, f32[264,256]{1,0:T(8,128)S(1)}, u32[]{:S(2)}, u32[]{:S(2)}) collective-permute-start(f32[264,256]{1,0:T(8,128)S(1)} %get-tuple-element.14), channel_id=1, source_target_pairs={{0,4},{4,0},{1,5},{5,1},{2,6},{6,2},{3,7},{7,3},{8,12},{12,8},{9,1... | collective-permute-start | bytes 811016 | tf_op jit(solution)/shard_map/ppermute | solution.py:247
  9.3 1.2 %collective-permute-done.got_ref = f32[264,256]{1,0:T(8,128)S(1)} collective-permute-done((f32[264,256]{1,0:T(8,128)S(1)}, f32[264,256]{1,0:T(8,128)S(1)}, u32[]{:S(2)}, u32[]{:S(2)}) %collective-permute-start) | collective-permute-done | bytes 270368 | tf_op jit(solution)/shard_map/ppermute | solution.py:247
  10.5 0.1 shard_map.85
  10.6 19.5 %all_to_all.10.msg_ref = f32[288,1,256]{2,1,0:T(1,128)S(1)} all-to-all(f32[288,1,256]{2,1,0:T(1,128)S(1)} %shard_map.85), channel_id=1, replica_groups=mesh['seq_y'=4,'seq_z'=8,'seq_c'=2,'batch'=4] {'seq_y','seq_z'}, dimensions={0} | all-to-all | bytes 589824 | tf_op jit(solution)/shard_map/all_to_all | solution.py:249
  30.1 0.1 shard_map.86
  30.2 16.5 %all_to_all.11 = f32[32,8,256]{2,1,0:T(8,128)S(1)} all-to-all(f32[32,8,256]{2,1,0:T(8,128)S(1)} %bitcast.4), channel_id=1, replica_groups=mesh['seq_y'=4,'seq_z'=8,'seq_c'=2,'batch'=4] {'seq_y','seq_z'}, dimensions={0} | all-to-all | bytes 524288 | tf_op jit(solution)/shard_map/all_to_all | solution.py:251
  46.8 0.1 shard_map.87
  46.8 3.7 %collective-permute-start.1 = (f32[256,256]{1,0:T(8,128)S(1)}, f32[256,256]{1,0:T(8,128)S(1)}, u32[]{:S(2)}, u32[]{:S(2)}) collective-permute-start(f32[256,256]{1,0:T(8,128)S(1)} %shard_map.87), channel_id=1, source_target_pairs={{0,4},{4,0},{1,5},{5,1},{2,6},{6,2},{3,7},{7,3},{8,12},{12,8},{9,1... | collective-permute-start | bytes 786440 | tf_op jit(solution)/shard_map/ppermute | solution.py:255
  50.6 0.0 copy-done.1
  50.6 0.0 copy-done.3
  50.6 0.0 copy-done.5
  50.6 0.0 copy-done.7
  50.6 1.7 %shard_map.88 = (f32[256,256]{1,0:T(8,128)S(1)}, f32[256,256]{1,0:T(8,128)S(1)}, f32[256,512]{1,0:T(8,128)S(1)}) custom-call(bf16[256,256]{1,0:T(8,128)(2,1)S(1)} %copy-done.5, bf16[256,256]{1,0:T(8,128)(2,1)S(1)} %copy-done.7, bf16[256,512]{1,0:T(8,128)(2,1)S(1)} %copy-done.1, bf16[256,512]{1,0:T(8,128)(2,1)S(1)} %copy-done.3, ...), custom_call_target="tpu_custom_call" | custom-call | flops 200000000 | bytes 2000000 | tf_op jit(solution)/shard_map/pallas_call | solution.py:227
  52.2 0.0 collective-permute-done.1.got_ref
  52.3 1.7 %shard_map.89 = (bf16[256,256]{1,0:T(8,128)(2,1)}, bf16[256,256]{1,0:T(8,128)(2,1)}, bf16[256,512]{1,0:T(8,128)(2,1)}, f32[256,256]{1,0:T(8,128)}) custom-call(bf16[256,256]{1,0:T(8,128)(2,1)S(1)} %copy-done.5, bf16[256,256]{1,0:T(8,128)(2,1)S(1)} %copy-done.7, bf16[256,512]{1,0:T(8,128)(2,1)S(1)} %copy-done.1, bf16[256,512]{1,0:T(8,128)(2,1)S(1)} %copy-done.3, ...), custom_call_target="tpu_custom_call" | custom-call | flops 1000000 | bytes 2000000 | tf_op jit(solution)/shard_map/pallas_call | solution.py:227
  (6 shorter events, 0.0 us)
Async XLA Ops:
  0.6 1.0 %copy-start = (bf16[256,512]{1,0:T(8,128)(2,1)S(1)}, bf16[256,512]{1,0:T(8,128)(2,1)}, u32[]{:S(2)}) copy-start(bf16[256,512]{1,0:T(8,128)(2,1)} %v_ref.5) | copy-start | bytes 786436
  1.6 0.9 %copy-start.2 = (bf16[256,512]{1,0:T(8,128)(2,1)S(1)}, bf16[256,512]{1,0:T(8,128)(2,1)}, u32[]{:S(2)}) copy-start(bf16[256,512]{1,0:T(8,128)(2,1)} %do_ref.5) | copy-start | bytes 786436
  2.5 0.9 %copy-start.4 = (bf16[256,256]{1,0:T(8,128)(2,1)S(1)}, bf16[256,256]{1,0:T(8,128)(2,1)}, u32[]{:S(2)}) copy-start(bf16[256,256]{1,0:T(8,128)(2,1)} %q_ref.5) | copy-start | bytes 393220
  3.4 0.9 %copy-start.6 = (bf16[256,256]{1,0:T(8,128)(2,1)S(1)}, bf16[256,256]{1,0:T(8,128)(2,1)}, u32[]{:S(2)}) copy-start(bf16[256,256]{1,0:T(8,128)(2,1)} %k_ref.5) | copy-start | bytes 393220
  4.3 0.9 %copy-start.8 = (f32[256,256]{1,0:T(8,128)S(1)}, f32[256,256]{1,0:T(8,128)}, u32[]{:S(2)}) copy-start(f32[256,256]{1,0:T(8,128)} %g_ref.1) | copy-start | bytes 786436
  6.1 4.4 %collective-permute-start = (f32[264,256]{1,0:T(8,128)S(1)}, f32[264,256]{1,0:T(8,128)S(1)}, u32[]{:S(2)}, u32[]{:S(2)}) collective-permute-start(f32[264,256]{1,0:T(8,128)S(1)} %get-tuple-element.14), channel_id=1, source_target_pairs={{0,4},{4,0},{1,5},{5,1},{2,6},{6,2},{3,7},{7,3},{8,12},{12,8},{9,1... | collective-permute-start | bytes 811016 | tf_op jit(solution)/shard_map/ppermute | solution.py:247
  46.7 3.8 %copy-start.1 = (bf16[256,512]{1,0:T(8,128)(2,1)S(1)}, bf16[256,512]{1,0:T(8,128)(2,1)}, u32[]{:S(2)}) copy-start(bf16[256,512]{1,0:T(8,128)(2,1)} %v_ref.5) | copy-start | bytes 786436
  46.7 3.8 %copy-start.3 = (bf16[256,512]{1,0:T(8,128)(2,1)S(1)}, bf16[256,512]{1,0:T(8,128)(2,1)}, u32[]{:S(2)}) copy-start(bf16[256,512]{1,0:T(8,128)(2,1)} %do_ref.5) | copy-start | bytes 786436
  46.7 3.8 %copy-start.5 = (bf16[256,256]{1,0:T(8,128)(2,1)S(1)}, bf16[256,256]{1,0:T(8,128)(2,1)}, u32[]{:S(2)}) copy-start(bf16[256,256]{1,0:T(8,128)(2,1)} %q_ref.5) | copy-start | bytes 393220
  46.7 3.8 %copy-start.7 = (bf16[256,256]{1,0:T(8,128)(2,1)S(1)}, bf16[256,256]{1,0:T(8,128)(2,1)}, u32[]{:S(2)}) copy-start(bf16[256,256]{1,0:T(8,128)(2,1)} %k_ref.5) | copy-start | bytes 393220
  46.8 5.4 %collective-permute-start.1 = (f32[256,256]{1,0:T(8,128)S(1)}, f32[256,256]{1,0:T(8,128)S(1)}, u32[]{:S(2)}, u32[]{:S(2)}) collective-permute-start(f32[256,256]{1,0:T(8,128)S(1)} %shard_map.87), channel_id=1, source_target_pairs={{0,4},{4,0},{1,5},{5,1},{2,6},{6,2},{3,7},{7,3},{8,12},{12,8},{9,1... | collective-permute-start | bytes 786440 | tf_op jit(solution)/shard_map/ppermute | solution.py:255

commit v2 on v1

v2 whole, which is shorter than its diff:
```python
import jax
import jax.numpy as jnp
from jax import lax
from jax.experimental import pallas as pl
from jax.experimental.pallas import tpu as pltpu
from jax.sharding import Mesh
from jax.sharding import PartitionSpec as P

H = 2
K = 128
V = 256
GROUP = 64
TOK = 256
HK = H * K
HV = H * V
Y, Z, CORES = 4, 8, 2
CHIPS = Y * Z
ROWS = V // CHIPS
MSG = ROWS + 1
CHIP_AXES = ("seq_y", "seq_z")
SPEC = P(("batch", "seq_y", "seq_z", "seq_c"), None)
F32 = jnp.float32
BF16 = jnp.bfloat16


def dot(left, right, dims):
    return lax.dot_general(left, right, (dims, ((), ())), preferred_element_type=F32)


def nn(left, right):
    return dot(left, right, ((1,), (0,)))


def nt(left, right):
    return dot(left, right, ((1,), (1,)))


def tn(left, right):
    return dot(left, right, ((0,), (0,)))


def split(x):
    hi = x.astype(BF16)
    return hi, (x - hi.astype(F32)).astype(BF16)


def pair(x):
    return jnp.concatenate(split(x), 1)


def folded(out):
    half = out.shape[1] // 2
    return out[:, :half] + out[:, half:]


def running_sum(x):
    rows = x.shape[0]
    r = lax.broadcasted_iota(jnp.int32, (rows, rows), 0)
    c = lax.broadcasted_iota(jnp.int32, (rows, rows), 1)
    ones = jnp.where(c <= r, 1.0, 0.0).astype(BF16)
    hi = x.astype(BF16)
    rest = x - hi.astype(F32)
    mid, lo = split(rest)
    return nn(ones, hi) + (nn(ones, mid) + nn(ones, lo))


def head(h, width):
    return slice(h * width, (h + 1) * width)


def at_head(h, width):
    return pl.ds(pl.multiple_of(h * width, width), width)


def halves(left, right):
    return jnp.concatenate((left, right), 1)


def block_ends(q_ref, k_ref, v_ref, do_ref, b_ref, out_ref, h):
    hk, hv = at_head(h, K), at_head(h, V)
    b = b_ref[:, hk]
    total = b_ref[TOK - 1 :, hk]
    out_ref[:V, :K] = folded(tn(v_ref[:, hv], pair(k_ref[:, hk].astype(F32) * jnp.exp(total - b))))
    out_ref[:V, K:] = folded(tn(do_ref[:, hv], pair(q_ref[:, hk].astype(F32) * jnp.exp(b))))


def first_kernel(
    q_hbm, k_hbm, v_hbm, do_hbm, g_hbm, q_ref, k_ref, v_ref, do_ref, b_ref, send_ref, g_ref, sems
):
    copies = [
        pltpu.make_async_copy(source, target, sems.at[n])
        for n, (source, target) in enumerate(
            ((g_hbm, g_ref), (k_hbm, k_ref), (v_hbm, v_ref), (q_hbm, q_ref), (do_hbm, do_ref))
        )
    ]
    for copy in copies:
        copy.start()
    copies[0].wait()
    b_ref[...] = running_sum(g_ref[...])
    for copy in copies[1:]:
        copy.wait()
    h = 1 - lax.axis_index("seq_c")
    block_ends(q_ref, k_ref, v_ref, do_ref, b_ref, send_ref, h)
    total = b_ref[TOK - 1 :, at_head(h, K)]
    send_ref[V:] = jnp.broadcast_to(halves(total, total), (8, HK))


def second_kernel(q_ref, k_ref, v_ref, do_ref, b_ref, own_ref):
    block_ends(q_ref, k_ref, v_ref, do_ref, b_ref, own_ref, lax.axis_index("seq_c"))


def lane_gates(b_ref, got_ref):
    core = lax.axis_index("seq_c")
    total = b_ref[TOK - 1 :, at_head(core, K)]
    mine = jnp.exp(halves(total, total))
    other = jnp.exp(got_ref[V : V + 1])
    forward = lax.broadcasted_iota(jnp.int32, (1, HK), 1) < K
    return mine, other, forward, core == 0


def pick(flag, forward, when_true, when_false):
    return jnp.where(jnp.logical_xor(forward, jnp.logical_not(flag)), when_true, when_false)


def message_kernel(own_ref, got_ref, b_ref, msg_ref, token_ref):
    mine, other, forward, first = lane_gates(b_ref, got_ref)
    own_gate = pick(first, forward, other, 1.0)
    got_gate = pick(first, forward, 1.0, mine)
    both = mine * other
    for i in range(CHIPS):
        rows = slice(i * ROWS, (i + 1) * ROWS)
        msg_ref[i * MSG : i * MSG + ROWS, 0, :] = own_ref[rows] * own_gate + got_ref[rows] * got_gate
        msg_ref[i * MSG + ROWS] = both
    token_ref[...] = jnp.zeros_like(token_ref)


def scan_kernel(msg_ref, _, out_ref):
    for order, lanes in ((range(CHIPS), slice(0, K)), (range(CHIPS - 1, -1, -1), slice(K, HK))):
        state = jnp.zeros((ROWS, K), F32)
        for i in order:
            out_ref[i * ROWS : (i + 1) * ROWS, lanes] = state
            gate = msg_ref[i * MSG + ROWS, :, lanes]
            state = gate * state + msg_ref[i * MSG : i * MSG + ROWS, 0, lanes]


def onward_kernel(own_ref, got_ref, b_ref, came_ref, send_ref, mine_ref):
    mine, other, forward, first = lane_gates(b_ref, got_ref)
    came = came_ref[...]
    send_ref[...] = came * pick(first, forward, mine, 1.0) + pick(
        first, forward, own_ref[...], 0.0
    )
    mine_ref[...] = came * pick(first, forward, 1.0, other) + pick(
        first, forward, 0.0, got_ref[:V]
    )


def inner_kernel(
    q_ref, k_ref, v_ref, do_ref, b_ref, _,
    dq_ref, dk_ref, dv_ref, rise_ref, tail_ref, kt_hi_ref, kt_lo_ref, token_ref,
):
    r = lax.broadcasted_iota(jnp.int32, (TOK, TOK), 0)
    c = lax.broadcasted_iota(jnp.int32, (TOK, TOK), 1)
    for h in range(H):
        hk, hv = head(h, K), head(h, V)
        q = q_ref[:, hk].astype(F32)
        k = k_ref[:, hk].astype(F32)
        b = b_ref[:, hk]
        dots = jnp.where(c <= r, nt(do_ref[:, hv], v_ref[:, hv]), 0.0)
        dots_t = jnp.where(c >= r, nt(v_ref[:, hv], do_ref[:, hv]), 0.0)
        p_hi, p_lo = split(dots)
        t_hi, t_lo = split(dots_t)
        dk = jnp.zeros((TOK, K), F32)
        dv = jnp.zeros((TOK, V), F32)
        for i in range(TOK // GROUP):
            rows = slice(i * GROUP, (i + 1) * GROUP)
            end = (i + 1) * GROUP
            upto = slice(0, end)
            start = b[i * GROUP - 1 : i * GROUP] if i else jnp.zeros((1, K), F32)
            rising = jnp.exp(b[rows] - start)
            falling = jnp.exp(start - b[upto])
            q_hi, q_lo = split(q[rows] * rising)
            k_hi, k_lo = split(k[upto] * falling)
            scores_t = nt(k_hi, q_hi) + (nt(k_hi, q_lo) + nt(k_lo, q_hi))
            rr = lax.broadcasted_iota(jnp.int32, (end, GROUP), 0)
            cc = lax.broadcasted_iota(jnp.int32, (end, GROUP), 1) + i * GROUP
            s_hi, s_lo = split(jnp.where(cc >= rr, scores_t, 0.0))
            k_both = halves(k_hi, k_lo)
            q_both = halves(q_hi, q_lo)
            dq_ref[rows, hk] = rising * (
                folded(nn(p_hi[rows, upto], k_both)) + nn(p_lo[rows, upto], k_hi)
            )
            dk_part = falling * (folded(nn(t_hi[upto, rows], q_both)) + nn(t_lo[upto, rows], q_hi))
            dv_part = nn(s_hi, do_ref[rows, hv]) + nn(s_lo, do_ref[rows, hv])
            if end < TOK:
                dk_part = jnp.concatenate((dk_part, jnp.zeros((TOK - end, K), F32)), 0)
                dv_part = jnp.concatenate((dv_part, jnp.zeros((TOK - end, V), F32)), 0)
            dk = dk + dk_part
            dv = dv + dv_part
        dk_ref[:, hk] = dk
        dv_ref[:, hv] = dv
        tail = jnp.exp(b[TOK - 1 :] - b)
        rise_ref[:, hk] = jnp.exp(b)
        tail_ref[:, hk] = tail
        kt_hi_ref[:, hk], kt_lo_ref[:, hk] = split(k * tail)
    token_ref[...] = jnp.zeros_like(token_ref)


def grads_kernel(
    own, q_ref, k_ref, v_ref, do_ref, b_ref, end_ref, in_ref, dqi_ref, dki_ref, dvi_ref,
    rise_ref, tail_ref, kt_hi_ref, kt_lo_ref, *rest,
):
    dq_hbm, dk_hbm, dv_hbm, dg_hbm, dq_ref, dk_ref, dv_ref, dg_ref, sems = rest[-9:]
    core = lax.axis_index("seq_c")
    h = core if own else 1 - core
    hk, hv = at_head(h, K), at_head(h, V)
    outs = ((dq_ref, dq_hbm, hk), (dk_ref, dk_hbm, hk), (dv_ref, dv_hbm, hv), (dg_ref, dg_hbm, hk))
    dq_out, dk_out, dv_out, dg_out = (
        pltpu.make_async_copy(source, target.at[:, lanes], sems.at[n])
        for n, (source, target, lanes) in enumerate(outs)
    )
    state = in_ref[:, :K]
    grad = in_ref[:, K:]
    g_hi, g_lo = split(grad)
    dq = dqi_ref[:, hk] + rise_ref[:, hk] * folded(nn(do_ref[:, hv], pair(state)))
    dk = dki_ref[:, hk] + tail_ref[:, hk] * folded(nn(v_ref[:, hv], halves(g_hi, g_lo)))
    dq_ref[...] = dq.astype(BF16)
    dq_out.start()
    dk_ref[...] = dk.astype(BF16)
    dk_out.start()
    t_hi, t_lo = kt_hi_ref[:, hk], kt_lo_ref[:, hk]
    dv = dvi_ref[:, hv] + (nt(halves(t_hi, t_lo), halves(g_hi, g_hi)) + nt(t_hi, g_lo))
    dv_ref[...] = dv.astype(BF16)
    dv_out.start()
    end_state = jnp.exp(b_ref[TOK - 1 :, hk]) * state + end_ref[:V, :K]
    later = jnp.sum(end_state * grad, axis=0, keepdims=True)
    terms = q_ref[:, hk].astype(F32) * dq - k_ref[:, hk].astype(F32) * dk
    r = lax.broadcasted_iota(jnp.int32, (TOK, TOK), 0)
    c = lax.broadcasted_iota(jnp.int32, (TOK, TOK), 1)
    ones = jnp.where(c >= r, 1.0, 0.0).astype(BF16)
    dg_ref[...] = folded(nn(ones, pair(terms))) + later
    dg_out.start()
    for copy in (dq_out, dk_out, dv_out, dg_out):
        copy.wait()


VMEM = pl.BlockSpec(memory_space=pltpu.VMEM)
HBM = pl.BlockSpec(memory_space=pltpu.HBM)
SQUARE = ((TOK, HK), F32)
SQUARE16 = ((TOK, HK), BF16)
WIDE16 = ((TOK, HV), BF16)
TOKEN = ((8, 128), F32)


def call(kernel, outs, *args, specs=None, out_specs=None, scratch=(), flops=1000000, alias=None):
    shapes = [jax.ShapeDtypeStruct(shape, dtype) for shape, dtype in outs]
    out = pl.pallas_call(
        kernel,
        out_shape=shapes,
        in_specs=specs or [VMEM] * len(args),
        out_specs=out_specs or [VMEM] * len(outs),
        scratch_shapes=list(scratch),
        input_output_aliases=alias or {},
        cost_estimate=pl.CostEstimate(flops=flops, bytes_accessed=2000000, transcendentals=0),
        compiler_params=pltpu.CompilerParams(vmem_limit_bytes=32 << 20),
    )(*args)
    return out if len(outs) > 1 else out[0]


SWAP = [(0, 1), (1, 0)]
GRAD_OUTS = [SQUARE16, SQUARE16, WIDE16, SQUARE]
GRAD_SCRATCH = [
    pltpu.VMEM((TOK, K), BF16),
    pltpu.VMEM((TOK, K), BF16),
    pltpu.VMEM((TOK, V), BF16),
    pltpu.VMEM((TOK, K), F32),
    pltpu.SemaphoreType.DMA((4,)),
]


def grads(own, args, into=()):
    def kernel(*refs):
        grads_kernel(own, *refs)

    return call(
        kernel,
        GRAD_OUTS,
        *args,
        *into,
        specs=[VMEM] * len(args) + [HBM] * len(into),
        out_specs=[HBM] * 4,
        scratch=GRAD_SCRATCH,
        flops=100000000,
        alias={len(args) + n: n for n in range(len(into))},
    )


def local(q, k, v, log_decay, do):
    q, k, v, do, log_decay = (pltpu.with_memory_space_constraint(x, pltpu.HBM) for x in (q, k, v, do, log_decay))
    q, k, v, do, b, send = call(
        first_kernel,
        [SQUARE16, SQUARE16, WIDE16, WIDE16, SQUARE, ((V + 8, HK), F32)],
        q, k, v, do, log_decay,
        specs=[HBM] * 5,
        scratch=[pltpu.VMEM((TOK, HK), F32), pltpu.SemaphoreType.DMA((5,))],
    )
    got = lax.ppermute(send, "seq_c", SWAP)
    own = call(second_kernel, [((V, HK), F32)], q, k, v, do, b, flops=100000000)
    msg, token = call(message_kernel, [((CHIPS * MSG, 1, HK), F32), TOKEN], own, got, b)
    msg = lax.all_to_all(msg, CHIP_AXES, 0, 0, tiled=True)
    *inner, token = call(
        inner_kernel,
        [SQUARE, SQUARE, ((TOK, HV), F32), SQUARE, SQUARE, SQUARE16, SQUARE16, TOKEN],
        q, k, v, do, b, token,
        flops=20000000000,
    )
    back = call(scan_kernel, [SQUARE], msg, token)
    came = lax.all_to_all(
        back.reshape(CHIPS, ROWS, HK), CHIP_AXES, 0, 0, tiled=True
    ).reshape(V, HK)
    onward, mine = call(onward_kernel, [SQUARE, SQUARE], own, got, b, came)
    theirs = lax.ppermute(onward, "seq_c", SWAP)
    half = grads(True, (q, k, v, do, b, own, mine, *inner))
    return grads(False, (q, k, v, do, b, send, theirs, *inner), half)


def solution(mesh):
    finer = Mesh(
        mesh.devices.reshape(Y, Z, CORES, mesh.shape["batch"]),
        ("seq_y", "seq_z", "seq_c", "batch"),
    )
    return jax.shard_map(
        local, mesh=finer, in_specs=(SPEC,) * 5, out_specs=(SPEC,) * 4, check_vma=False
    )
```

time: 54.3 us -> 50.4 us (0.928)
  blocking collectives: 36 us -> 16.5 us
  starting transfers between devices: 7.02 us -> 16.5 us
  waiting for transfers between devices: 1.18 us -> 8.06 us
  local copies, waits for them, and re-layouts: 4.67 us -> 1.32 us
  Pallas kernels: 4.45 us -> 7.02 us
    all_to_all x1 -> x0, blocking collectives: 19.5 us -> none  [local(): msg = lax.all_to_all(msg, CHIP_AXES, 0, 0, tiled=True)]
    all_to_all x0 -> x1, starting transfers between devices: none -> 9.5 us  [local(): msg = lax.all_to_all(msg, CHIP_AXES, 0, 0, tiled=True)]
    all_to_all x0 -> x1, waiting for transfers between devices: none -> 7.19 us  [local(): msg = lax.all_to_all(msg, CHIP_AXES, 0, 0, tiled=True)]
    unnamed x18 -> x12, local copies, waits for them, and re-layouts: 4.67 us -> 1.32 us
    pallas_call x6 -> x8, Pallas kernels: 4.45 us -> 7.02 us  [call(): pl.pallas_call(kernel, out_shape=shapes, in_specs=specs or [VMEM] * len(a...]
  transfers between devices with their start and end apart: 2 -> 3, of which waited for: 1 -> 2; matrix products, arithmetic and copies ran while one was open for 0% -> 0% of each run, Pallas kernels for 3% -> 6%
where the time goes in v2:
time: 50.4 us; the launch traced here: 50.2 us
  starting transfers between devices  16.5 us (33%)
  blocking collectives  16.5 us (33%)
  waiting for transfers between devices  8.06 us (16%)
  Pallas kernels  7.02 us (14%)
  local copies, waits for them, and re-layouts  1.32 us (3%)
  between operations  0.72 us (1%)
    all_to_all x1, blocking collectives, local(): lax.all_to_all(back.reshape(CHIPS, ROWS, HK), CHIP_AXES, 0, 0, tiled=True)  16.5 us
    all_to_all x1, starting transfers between devices, local(): msg = lax.all_to_all(msg, CHIP_AXES, 0, 0, tiled=True)  9.5 us
    all_to_all x1, waiting for transfers between devices, local(): msg = lax.all_to_all(msg, CHIP_AXES, 0, 0, tiled=True)  7.19 us
    pallas_call x8, Pallas kernels, call(): pl.pallas_call(kernel, out_shape=shapes, in_specs=specs or [VMEM] * len(a...  7.02 us
    ppermute x1, starting transfers between devices, local(): theirs = lax.ppermute(onward, 'seq_c', SWAP)  3.76 us
    ppermute x1, starting transfers between devices, local(): got = lax.ppermute(send, 'seq_c', SWAP)  3.29 us
    unnamed x12, local copies, waits for them, and re-layouts  1.32 us
  transfers between devices with their start and end apart: 3, of which 2 were waited for; matrix products, arithmetic and copies ran while one was open for 0% of the time, Pallas kernels for 6%

profile of v2, /device:TPU:1, one launch (start us, length us, event | category | flops | bytes accessed | tf_op | source)
XLA Modules:
  0.0 50.2 jit_solution(13996385620640647191)
XLA Ops:
  0.6 1.7 %shard_map.84 = (bf16[256,256]{1,0:T(8,128)(2,1)S(1)}, bf16[256,256]{1,0:T(8,128)(2,1)S(1)}, bf16[256,512]{1,0:T(8,128)(2,1)S(1)}, bf16[256,512]{1,0:T(8,128)(2,...) custom-call(bf16[256,256]{1,0:T(8,128)(2,1)} %q_hbm.1, bf16[256,256]{1,0:T(8,128)(2,1)} %k_hbm.1, ...), custom_call_target="tpu_custom_call" | custom-call | flops 1000000 | bytes 2000000 | tf_op jit(solution)/shard_map/pallas_call | solution.py:256
  2.3 0.0 copy-start.4
  2.3 3.3 %collective-permute-start = (f32[264,256]{1,0:T(8,128)S(1)}, f32[264,256]{1,0:T(8,128)S(1)}, u32[]{:S(2)}, u32[]{:S(2)}) collective-permute-start(f32[264,256]{1,0:T(8,128)S(1)} %get-tuple-element.31.refs_5_), channel_id=1, source_target_pairs={{0,4},{4,0},{1,5},{5,1},{2,6},{6,2},{3,7},{7,3},{8,12},{12,8},{9,1... | collective-permute-start | bytes 811016 | tf_op jit(solution)/shard_map/ppermute | solution.py:306
  5.6 0.3 shard_map.85.own_ref.refs_5_
  5.9 0.0 copy-done.4
  5.9 0.9 %collective-permute-done.got_ref = f32[264,256]{1,0:T(8,128)S(1)} collective-permute-done((f32[264,256]{1,0:T(8,128)S(1)}, f32[264,256]{1,0:T(8,128)S(1)}, u32[]{:S(2)}, u32[]{:S(2)}) %collective-permute-start) | collective-permute-done | bytes 270368 | tf_op jit(solution)/shard_map/ppermute | solution.py:306
  6.8 0.8 %shard_map.86 = (f32[288,1,256]{2,1,0:T(1,128)}, f32[8,128]{1,0:T(8,128)S(1)}) custom-call(f32[256,256]{1,0:T(8,128)S(1)} %shard_map.85.own_ref.refs_5_, f32[264,256]{1,0:T(8,128)S(1)} %collective-permute-done.got_ref, f32[256,256]{1,0:T(8,128)S(1)} %get-tuple-element.30.b_ref.refs_4_), custom_call_target="tpu_custom_call" | custom-call | flops 1000000 | bytes 2000000 | tf_op jit(solution)/shard_map/pallas_call | solution.py:256
  7.6 9.5 %all-to-all-start = ((f32[288,1,256]{2,1,0:T(1,128)}), f32[288,1,256]{2,1,0:T(1,128)S(1)}, u32[]{:S(2)}, u32[]{:S(2)}) async-start(f32[288,1,256]{2,1,0:T(1,128)} %get-tuple-element.32), calls=%async_computation | async-start | bytes 589824 | tf_op jit(solution)/shard_map/all_to_all | solution.py:309
  17.1 1.7 %shard_map.87 = (f32[256,256]{1,0:T(8,128)S(1)}, f32[256,256]{1,0:T(8,128)S(1)}, f32[256,512]{1,0:T(8,128)S(1)}, f32[256,256]{1,0:T(8,128)S(1)}, f32[256,256]{1,...) custom-call(bf16[256,256]{1,0:T(8,128)(2,1)S(1)} %get-tuple-element.26.q_ref.refs_0, ...), custom_call_target="tpu_custom_call" | custom-call | flops 20000000000 | bytes 2000000 | tf_op jit(solution)/shard_map/pallas_call | solution.py:256
  18.8 0.0 copy-start
  18.8 0.6 %copy-done = bf16[256,256]{1,0:T(8,128)(2,1)} copy-done((bf16[256,256]{1,0:T(8,128)(2,1)}, bf16[256,256]{1,0:T(8,128)(2,1)S(1)}, u32[]{:S(2)}) %copy-start) | copy-done | bytes 131096
  19.5 0.0 copy-start.2
  19.5 0.7 %copy-done.2 = bf16[256,256]{1,0:T(8,128)(2,1)} copy-done((bf16[256,256]{1,0:T(8,128)(2,1)}, bf16[256,256]{1,0:T(8,128)(2,1)S(1)}, u32[]{:S(2)}) %copy-start.2) | copy-done | bytes 131096
  20.1 7.2 %all-to-all-done.msg_ref = f32[288,1,256]{2,1,0:T(1,128)S(1)} async-done(((f32[288,1,256]{2,1,0:T(1,128)}), f32[288,1,256]{2,1,0:T(1,128)S(1)}, u32[]{:S(2)}, u32[]{:S(2)}) %all-to-all-start) | async-done | bytes 294944 | tf_op jit(solution)/shard_map/all_to_all | solution.py:309
  27.3 0.1 shard_map.88
  27.4 16.5 %all_to_all.10 = f32[32,8,256]{2,1,0:T(8,128)S(1)} all-to-all(f32[32,8,256]{2,1,0:T(8,128)S(1)} %bitcast.2), channel_id=1, replica_groups=mesh['seq_y'=4,'seq_z'=8,'seq_c'=2,'batch'=4] {'seq_y','seq_z'}, dimensions={0} | all-to-all | bytes 524288 | tf_op jit(solution)/shard_map/all_to_all | solution.py:317
  44.0 0.1 shard_map.89
  44.0 3.8 %collective-permute-start.1 = (f32[256,256]{1,0:T(8,128)S(1)}, f32[256,256]{1,0:T(8,128)S(1)}, u32[]{:S(2)}, u32[]{:S(2)}) collective-permute-start(f32[256,256]{1,0:T(8,128)S(1)} %get-tuple-element.35), channel_id=1, source_target_pairs={{0,4},{4,0},{1,5},{5,1},{2,6},{6,2},{3,7},{7,3},{8,12},{12,8},{9,1... | collective-permute-start | bytes 786440 | tf_op jit(solution)/shard_map/ppermute | solution.py:321
  47.8 0.0 copy-done.1
  47.8 0.0 copy-done.3
  47.8 1.2 %shard_map.90 = (bf16[256,256]{1,0:T(8,128)(2,1)}, bf16[256,256]{1,0:T(8,128)(2,1)}, bf16[256,512]{1,0:T(8,128)(2,1)}, f32[256,256]{1,0:T(8,128)}) custom-call(bf16[256,256]{1,0:T(8,128)(2,1)S(1)} %get-tuple-element.26.q_ref.refs_0_, bf16[256,256]{1,0:T(8,128)(2,1)S(1)} %get-tuple-element.27.k_ref.refs_1_, ...), custom_call_target="tpu_custom_call" | custom-call | flops 100000000 | bytes 2000000 | tf_op jit(solution)/shard_map/pallas_call | solution.py:256
  49.0 0.0 collective-permute-done.1.refs_6_
  49.0 0.0 copy-done.5
  49.0 1.2 %shard_map.91 = (bf16[256,256]{1,0:T(8,128)(2,1)}, bf16[256,256]{1,0:T(8,128)(2,1)}, bf16[256,512]{1,0:T(8,128)(2,1)}, f32[256,256]{1,0:T(8,128)}) custom-call(bf16[256,256]{1,0:T(8,128)(2,1)S(1)} %get-tuple-element.26.q_ref.refs_0_, ...), custom_call_target="tpu_custom_call", output_to_operand_aliasing={{0}: (14, {}), {1}: (15, {}), {2}: (16, {}), {3}: (17, {})} | custom-call | flops 100000000 | bytes 2000000 | tf_op jit(solution)/shard_map/pallas_call | solution.py:256
  (3 shorter events, 0.0 us)
Async XLA Ops:
  2.3 3.6 %copy-start.4 = (f32[264,256]{1,0:T(8,128)}, f32[264,256]{1,0:T(8,128)S(1)}, u32[]{:S(2)}) copy-start(f32[264,256]{1,0:T(8,128)S(1)} %get-tuple-element.31.refs_5_) | copy-start | bytes 811012
  2.3 4.5 %collective-permute-start = (f32[264,256]{1,0:T(8,128)S(1)}, f32[264,256]{1,0:T(8,128)S(1)}, u32[]{:S(2)}, u32[]{:S(2)}) collective-permute-start(f32[264,256]{1,0:T(8,128)S(1)} %get-tuple-element.31.refs_5_), channel_id=1, source_target_pairs={{0,4},{4,0},{1,5},{5,1},{2,6},{6,2},{3,7},{7,3},{8,12},{12,8},{9,1... | collective-permute-start | bytes 811016 | tf_op jit(solution)/shard_map/ppermute | solution.py:306
  7.6 19.7 %all-to-all-start = ((f32[288,1,256]{2,1,0:T(1,128)}), f32[288,1,256]{2,1,0:T(1,128)S(1)}, u32[]{:S(2)}, u32[]{:S(2)}) async-start(f32[288,1,256]{2,1,0:T(1,128)} %get-tuple-element.32), calls=%async_computation | async-start | bytes 589824 | tf_op jit(solution)/shard_map/all_to_all | solution.py:309
  18.8 0.7 %copy-start = (bf16[256,256]{1,0:T(8,128)(2,1)}, bf16[256,256]{1,0:T(8,128)(2,1)S(1)}, u32[]{:S(2)}) copy-start(bf16[256,256]{1,0:T(8,128)(2,1)S(1)} %get-tuple-element.41.refs_12_) | copy-start | bytes 393220
  19.5 0.7 %copy-start.2 = (bf16[256,256]{1,0:T(8,128)(2,1)}, bf16[256,256]{1,0:T(8,128)(2,1)S(1)}, u32[]{:S(2)}) copy-start(bf16[256,256]{1,0:T(8,128)(2,1)S(1)} %get-tuple-element.42.refs_13_) | copy-start | bytes 393220
  43.9 3.8 %copy-start.1 = (bf16[256,256]{1,0:T(8,128)(2,1)S(1)}, bf16[256,256]{1,0:T(8,128)(2,1)}, u32[]{:S(2)}) copy-start(bf16[256,256]{1,0:T(8,128)(2,1)} %copy-done) | copy-start | bytes 393220
  43.9 3.8 %copy-start.3 = (bf16[256,256]{1,0:T(8,128)(2,1)S(1)}, bf16[256,256]{1,0:T(8,128)(2,1)}, u32[]{:S(2)}) copy-start(bf16[256,256]{1,0:T(8,128)(2,1)} %copy-done.2) | copy-start | bytes 393220
  44.0 4.9 %collective-permute-start.1 = (f32[256,256]{1,0:T(8,128)S(1)}, f32[256,256]{1,0:T(8,128)S(1)}, u32[]{:S(2)}, u32[]{:S(2)}) collective-permute-start(f32[256,256]{1,0:T(8,128)S(1)} %get-tuple-element.35), channel_id=1, source_target_pairs={{0,4},{4,0},{1,5},{5,1},{2,6},{6,2},{3,7},{7,3},{8,12},{12,8},{9,1... | collective-permute-start | bytes 786440 | tf_op jit(solution)/shard_map/ppermute | solution.py:321
  47.8 1.2 %copy-start.5 = (f32[264,256]{1,0:T(8,128)S(1)}, f32[264,256]{1,0:T(8,128)}, u32[]{:S(2)}) copy-start(f32[264,256]{1,0:T(8,128)} %copy-done.4) | copy-start | bytes 811012

commit v3 on v2

v3 whole, which is shorter than its diff:
```python
import jax
import jax.numpy as jnp
from jax import lax
from jax.experimental import pallas as pl
from jax.experimental.pallas import tpu as pltpu
from jax.sharding import Mesh
from jax.sharding import PartitionSpec as P

H = 2
K = 128
V = 256
GROUP = 64
TOK = 256
HK = H * K
HV = H * V
Y, Z, CORES = 4, 8, 2
CHIPS = Y * Z
ROWS = V // CHIPS
MSG = ROWS + 1
CHIP_AXES = ("seq_y", "seq_z")
SPEC = P(("batch", "seq_y", "seq_z", "seq_c"), None)
F32 = jnp.float32
BF16 = jnp.bfloat16


def dot(left, right, dims):
    return lax.dot_general(left, right, (dims, ((), ())), preferred_element_type=F32)


def nn(left, right):
    return dot(left, right, ((1,), (0,)))


def nt(left, right):
    return dot(left, right, ((1,), (1,)))


def tn(left, right):
    return dot(left, right, ((0,), (0,)))


def split(x):
    hi = x.astype(BF16)
    return hi, (x - hi.astype(F32)).astype(BF16)


def pair(x):
    return jnp.concatenate(split(x), 1)


def folded(out):
    half = out.shape[1] // 2
    return out[:, :half] + out[:, half:]


def running_sum(x):
    rows = x.shape[0]
    r = lax.broadcasted_iota(jnp.int32, (rows, rows), 0)
    c = lax.broadcasted_iota(jnp.int32, (rows, rows), 1)
    ones = jnp.where(c <= r, 1.0, 0.0).astype(BF16)
    hi = x.astype(BF16)
    rest = x - hi.astype(F32)
    mid, lo = split(rest)
    return nn(ones, hi) + (nn(ones, mid) + nn(ones, lo))


def head(h, width):
    return slice(h * width, (h + 1) * width)


def at_head(h, width):
    return pl.ds(pl.multiple_of(h * width, width), width)


def halves(left, right):
    return jnp.concatenate((left, right), 1)


def block_ends(q_ref, k_ref, v_ref, do_ref, b_ref, out_ref, h):
    hk, hv = at_head(h, K), at_head(h, V)
    b = b_ref[:, hk]
    total = b_ref[TOK - 1 :, hk]
    out_ref[:V, :K] = folded(tn(v_ref[:, hv], pair(k_ref[:, hk].astype(F32) * jnp.exp(total - b))))
    out_ref[:V, K:] = folded(tn(do_ref[:, hv], pair(q_ref[:, hk].astype(F32) * jnp.exp(b))))


def first_kernel(
    q_hbm, k_hbm, v_hbm, do_hbm, g_hbm, q_ref, k_ref, v_ref, do_ref, b_ref, send_ref, g_ref, sems
):
    copies = [
        pltpu.make_async_copy(source, target, sems.at[n])
        for n, (source, target) in enumerate(
            ((g_hbm, g_ref), (k_hbm, k_ref), (v_hbm, v_ref), (q_hbm, q_ref), (do_hbm, do_ref))
        )
    ]
    for copy in copies:
        copy.start()
    copies[0].wait()
    b_ref[...] = running_sum(g_ref[...])
    for copy in copies[1:]:
        copy.wait()
    h = 1 - lax.axis_index("seq_c")
    block_ends(q_ref, k_ref, v_ref, do_ref, b_ref, send_ref, h)
    total = b_ref[TOK - 1 :, at_head(h, K)]
    send_ref[V:] = jnp.broadcast_to(halves(total, total), (8, HK))


def inner_pairs(q_ref, k_ref, v_ref, do_ref, b_ref, h, dq_ref, dk_ref, dv_ref):
    hk, hv = at_head(h, K), at_head(h, V)
    r = lax.broadcasted_iota(jnp.int32, (TOK, TOK), 0)
    c = lax.broadcasted_iota(jnp.int32, (TOK, TOK), 1)
    q = q_ref[:, hk].astype(F32)
    k = k_ref[:, hk].astype(F32)
    b = b_ref[:, hk]
    v = v_ref[:, hv]
    do = do_ref[:, hv]
    p_hi, p_lo = split(jnp.where(c <= r, nt(do, v), 0.0))
    t_hi, t_lo = split(jnp.where(c >= r, nt(v, do), 0.0))
    dk = jnp.zeros((TOK, K), F32)
    dv = jnp.zeros((TOK, V), F32)
    for i in range(TOK // GROUP):
        rows = slice(i * GROUP, (i + 1) * GROUP)
        end = (i + 1) * GROUP
        upto = slice(0, end)
        start = b[i * GROUP - 1 : i * GROUP] if i else jnp.zeros((1, K), F32)
        rising = jnp.exp(b[rows] - start)
        falling = jnp.exp(start - b[upto])
        q_hi, q_lo = split(q[rows] * rising)
        k_hi, k_lo = split(k[upto] * falling)
        scores_t = nt(k_hi, q_hi) + (nt(k_hi, q_lo) + nt(k_lo, q_hi))
        rr = lax.broadcasted_iota(jnp.int32, (end, GROUP), 0)
        cc = lax.broadcasted_iota(jnp.int32, (end, GROUP), 1) + i * GROUP
        s_hi, s_lo = split(jnp.where(cc >= rr, scores_t, 0.0))
        dq_ref[rows] = rising * (
            folded(nn(p_hi[rows, upto], halves(k_hi, k_lo))) + nn(p_lo[rows, upto], k_hi)
        )
        dk_part = falling * (
            folded(nn(t_hi[upto, rows], halves(q_hi, q_lo))) + nn(t_lo[upto, rows], q_hi)
        )
        dv_part = nn(s_hi, do[rows]) + nn(s_lo, do[rows])
        if end < TOK:
            dk_part = jnp.concatenate((dk_part, jnp.zeros((TOK - end, K), F32)), 0)
            dv_part = jnp.concatenate((dv_part, jnp.zeros((TOK - end, V), F32)), 0)
        dk = dk + dk_part
        dv = dv + dv_part
    dk_ref[...] = dk
    dv_ref[...] = dv


def outer_gates(k_ref, b_ref, h, rise_ref, tail_ref, kt_ref):
    hk = at_head(h, K)
    b = b_ref[:, hk]
    tail = jnp.exp(b_ref[TOK - 1 :, hk] - b)
    rise_ref[...] = jnp.exp(b)
    tail_ref[...] = tail
    kt_ref[...] = pair(k_ref[:, hk].astype(F32) * tail)


def second_kernel(q_ref, k_ref, v_ref, do_ref, b_ref, own_ref, *inner_refs):
    core = lax.axis_index("seq_c")
    block_ends(q_ref, k_ref, v_ref, do_ref, b_ref, own_ref, core)
    outer_gates(k_ref, b_ref, core, *inner_refs[3:])
    inner_pairs(q_ref, k_ref, v_ref, do_ref, b_ref, core, *inner_refs[:3])


def lane_gates(b_ref, got_ref):
    core = lax.axis_index("seq_c")
    total = b_ref[TOK - 1 :, at_head(core, K)]
    mine = jnp.exp(halves(total, total))
    other = jnp.exp(got_ref[V : V + 1])
    forward = lax.broadcasted_iota(jnp.int32, (1, HK), 1) < K
    return mine, other, forward, core == 0


def pick(flag, forward, when_true, when_false):
    return jnp.where(jnp.logical_xor(forward, jnp.logical_not(flag)), when_true, when_false)


def message_kernel(own_ref, got_ref, b_ref, msg_ref):
    mine, other, forward, first = lane_gates(b_ref, got_ref)
    own_gate = pick(first, forward, other, 1.0)
    got_gate = pick(first, forward, 1.0, mine)
    both = mine * other
    for i in range(CHIPS):
        rows = slice(i * ROWS, (i + 1) * ROWS)
        msg_ref[i * MSG : i * MSG + ROWS, 0, :] = own_ref[rows] * own_gate + got_ref[rows] * got_gate
        msg_ref[i * MSG + ROWS] = both


def scan_kernel(msg_ref, out_ref):
    for order, lanes in ((range(CHIPS), slice(0, K)), (range(CHIPS - 1, -1, -1), slice(K, HK))):
        state = jnp.zeros((ROWS, K), F32)
        for i in order:
            out_ref[i * ROWS : (i + 1) * ROWS, lanes] = state
            gate = msg_ref[i * MSG + ROWS, :, lanes]
            state = gate * state + msg_ref[i * MSG : i * MSG + ROWS, 0, lanes]


def onward_kernel(own_ref, got_ref, b_ref, came_ref, send_ref, mine_ref):
    mine, other, forward, first = lane_gates(b_ref, got_ref)
    came = came_ref[...]
    send_ref[...] = came * pick(first, forward, mine, 1.0) + pick(
        first, forward, own_ref[...], 0.0
    )
    mine_ref[...] = came * pick(first, forward, 1.0, other) + pick(
        first, forward, 0.0, got_ref[:V]
    )


def head_grads(
    h, q_ref, k_ref, v_ref, do_ref, b_ref, end_ref, in_ref,
    dqi_ref, dki_ref, dvi_ref, rise_ref, tail_ref, kt_ref, dq_ref, dk_ref, dv_ref, dg_ref, stored,
):
    hk, hv = at_head(h, K), at_head(h, V)
    state = in_ref[:, :K]
    grad = in_ref[:, K:]
    g_hi, g_lo = split(grad)
    dq = dqi_ref[...] + rise_ref[...] * folded(nn(do_ref[:, hv], pair(state)))
    dk = dki_ref[...] + tail_ref[...] * folded(nn(v_ref[:, hv], halves(g_hi, g_lo)))
    dq_ref[...] = dq.astype(BF16)
    stored(0)
    dk_ref[...] = dk.astype(BF16)
    stored(1)
    dv = dvi_ref[...] + (nt(kt_ref[...], halves(g_hi, g_hi)) + nt(kt_ref[:, :K], g_lo))
    dv_ref[...] = dv.astype(BF16)
    stored(2)
    end_state = jnp.exp(b_ref[TOK - 1 :, hk]) * state + end_ref[:V, :K]
    later = jnp.sum(end_state * grad, axis=0, keepdims=True)
    terms = q_ref[:, hk].astype(F32) * dq - k_ref[:, hk].astype(F32) * dk
    r = lax.broadcasted_iota(jnp.int32, (TOK, TOK), 0)
    c = lax.broadcasted_iota(jnp.int32, (TOK, TOK), 1)
    ones = jnp.where(c >= r, 1.0, 0.0).astype(BF16)
    dg_ref[...] = folded(nn(ones, pair(terms))) + later
    stored(3)


def own_grads_kernel(q_ref, k_ref, v_ref, do_ref, b_ref, own_ref, in_ref, *rest):
    core = lax.axis_index("seq_c")
    args = (q_ref, k_ref, v_ref, do_ref, b_ref)
    head_grads(core, *args, own_ref, in_ref, *rest[:6], *rest[6:10], lambda n: None)
    outer_gates(k_ref, b_ref, 1 - core, *rest[13:])
    inner_pairs(*args, 1 - core, *rest[10:13])


def final_kernel(q_ref, k_ref, v_ref, do_ref, b_ref, sent_ref, in_ref, *rest):
    inner_refs, mine, outs, theirs, sems = rest[:6], rest[6:10], rest[10:14], rest[14:18], rest[18]
    core = lax.axis_index("seq_c")
    widths = (K, K, V, K)

    def copies(sources, h, base):
        return [
            pltpu.make_async_copy(source, out.at[:, at_head(h, width)], sems.at[base + n])
            for n, (source, out, width) in enumerate(zip(sources, outs, widths))
        ]

    first = copies(mine, core, 0)
    second = copies(theirs, 1 - core, 4)
    for copy in first:
        copy.start()
    head_grads(
        1 - core, q_ref, k_ref, v_ref, do_ref, b_ref, sent_ref, in_ref, *inner_refs, *theirs,
        lambda n: second[n].start(),
    )
    for copy in first + second:
        copy.wait()


VMEM = pl.BlockSpec(memory_space=pltpu.VMEM)
HBM = pl.BlockSpec(memory_space=pltpu.HBM)
SQUARE = ((TOK, HK), F32)
SQUARE16 = ((TOK, HK), BF16)
WIDE16 = ((TOK, HV), BF16)
HALF = ((TOK, K), F32)
INNER = [HALF, HALF, ((TOK, V), F32), HALF, HALF, ((TOK, 2 * K), BF16)]
HALF_GRADS = [((TOK, K), BF16), ((TOK, K), BF16), ((TOK, V), BF16), HALF]


def call(kernel, outs, *args, specs=None, out_specs=None, scratch=(), flops=1000000):
    shapes = [jax.ShapeDtypeStruct(shape, dtype) for shape, dtype in outs]
    out = pl.pallas_call(
        kernel,
        out_shape=shapes,
        in_specs=specs or [VMEM] * len(args),
        out_specs=out_specs or [VMEM] * len(outs),
        scratch_shapes=list(scratch),
        cost_estimate=pl.CostEstimate(flops=flops, bytes_accessed=2000000, transcendentals=0),
        compiler_params=pltpu.CompilerParams(vmem_limit_bytes=32 << 20),
    )(*args)
    return out if len(outs) > 1 else out[0]


SWAP = [(0, 1), (1, 0)]


def local(q, k, v, log_decay, do):
    q, k, v, do, log_decay = (
        pltpu.with_memory_space_constraint(x, pltpu.HBM) for x in (q, k, v, do, log_decay)
    )
    q, k, v, do, b, send = call(
        first_kernel,
        [SQUARE16, SQUARE16, WIDE16, WIDE16, SQUARE, ((V + 8, HK), F32)],
        q, k, v, do, log_decay,
        specs=[HBM] * 5,
        scratch=[pltpu.VMEM((TOK, HK), F32), pltpu.SemaphoreType.DMA((5,))],
    )
    got = lax.ppermute(send, "seq_c", SWAP)
    own, *inner = call(second_kernel, [SQUARE, *INNER], q, k, v, do, b, flops=100000000)
    msg = call(message_kernel, [((CHIPS * MSG, 1, HK), F32)], own, got, b)
    msg = lax.all_to_all(msg, CHIP_AXES, 0, 0, tiled=True)
    back = call(scan_kernel, [SQUARE], msg)
    came = lax.all_to_all(
        back.reshape(CHIPS, ROWS, HK), CHIP_AXES, 0, 0, tiled=True
    ).reshape(V, HK)
    onward, mine = call(onward_kernel, [SQUARE, SQUARE], own, got, b, came)
    theirs = lax.ppermute(onward, "seq_c", SWAP)
    done = call(
        own_grads_kernel,
        HALF_GRADS + INNER,
        q, k, v, do, b, own, mine, *inner,
        flops=100000000,
    )
    return call(
        final_kernel,
        [SQUARE16, SQUARE16, WIDE16, SQUARE],
        q, k, v, do, b, send, theirs, *done[4:], *done[:4],
        out_specs=[HBM] * 4,
        scratch=[pltpu.VMEM(*out) for out in HALF_GRADS] + [pltpu.SemaphoreType.DMA((8,))],
    )


def solution(mesh):
    finer = Mesh(
        mesh.devices.reshape(Y, Z, CORES, mesh.shape["batch"]),
        ("seq_y", "seq_z", "seq_c", "batch"),
    )
    return jax.shard_map(
        local, mesh=finer, in_specs=(SPEC,) * 5, out_specs=(SPEC,) * 4, check_vma=False
    )
```

time: 50.4 us -> 49.5 us (0.982)
  blocking collectives: 16.5 us -> 36 us
  starting transfers between devices: 16.5 us -> 7.04 us
  waiting for transfers between devices: 8.06 us -> 0.12 us
  Pallas kernels: 7.02 us -> 5.52 us
  local copies, waits for them, and re-layouts: 1.32 us -> 0 us
    all_to_all x0 -> x1, blocking collectives: none -> 19.5 us  [local(): msg = lax.all_to_all(msg, CHIP_AXES, 0, 0, tiled=True)]
    all_to_all x1 -> x0, starting transfers between devices: 9.5 us -> none  [local(): msg = lax.all_to_all(msg, CHIP_AXES, 0, 0, tiled=True)]
    all_to_all x1 -> x0, waiting for transfers between devices: 7.19 us -> none  [local(): msg = lax.all_to_all(msg, CHIP_AXES, 0, 0, tiled=True)]
    pallas_call x8 -> x7, Pallas kernels: 7.02 us -> 5.52 us  [call(): pl.pallas_call(kernel, out_shape=shapes, in_specs=specs or [VMEM] * len(a...]
    unnamed x12 -> x0, local copies, waits for them, and re-layouts: 1.32 us -> none
    ppermute x1, waiting for transfers between devices: 0.87 us -> 0.11 us  [local(): got = lax.ppermute(send, 'seq_c', SWAP)]
  transfers between devices with their start and end apart: 3 -> 2, of which waited for: 2 -> 1; matrix products, arithmetic and copies ran while one was open for 0% -> 0% of each run, Pallas kernels for 6% -> 5%
where the time goes in v3:
time: 49.5 us; the launch traced here: 49.4 us
  blocking collectives  36 us (73%)
  starting transfers between devices  7.04 us (14%)
  Pallas kernels  5.52 us (11%)
  between operations  0.68 us (1%)
    all_to_all x1, blocking collectives, local(): msg = lax.all_to_all(msg, CHIP_AXES, 0, 0, tiled=True)  19.5 us
    all_to_all x1, blocking collectives, local(): lax.all_to_all(back.reshape(CHIPS, ROWS, HK), CHIP_AXES, 0, 0, tiled=True)  16.5 us
    pallas_call x7, Pallas kernels, call(): pl.pallas_call(kernel, out_shape=shapes, in_specs=specs or [VMEM] * len(a...  5.52 us
    ppermute x1, starting transfers between devices, local(): theirs = lax.ppermute(onward, 'seq_c', SWAP)  3.75 us
    ppermute x1, starting transfers between devices, local(): got = lax.ppermute(send, 'seq_c', SWAP)  3.29 us
  transfers between devices with their start and end apart: 2, of which 1 were waited for; matrix products, arithmetic and copies ran while one was open for 0% of the time, Pallas kernels for 5%

profile of v3, /device:TPU:1, one launch (start us, length us, event | category | flops | bytes accessed | tf_op | source)
XLA Modules:
  0.0 49.4 jit_solution(647431933436352963)
XLA Ops:
  0.6 1.7 %shard_map.84 = (bf16[256,256]{1,0:T(8,128)(2,1)S(1)}, bf16[256,256]{1,0:T(8,128)(2,1)S(1)}, bf16[256,512]{1,0:T(8,128)(2,1)S(1)}, bf16[256,512]{1,0:T(8,128)(2,...) custom-call(bf16[256,256]{1,0:T(8,128)(2,1)} %q_hbm.1, bf16[256,256]{1,0:T(8,128)(2,1)} %k_hbm.1, ...), custom_call_target="tpu_custom_call" | custom-call | flops 1000000 | bytes 2000000 | tf_op jit(solution)/shard_map/pallas_call | solution.py:280
  2.3 3.3 %collective-permute-start = (f32[264,256]{1,0:T(8,128)S(1)}, f32[264,256]{1,0:T(8,128)S(1)}, u32[]{:S(2)}, u32[]{:S(2)}) collective-permute-start(f32[264,256]{1,0:T(8,128)S(1)} %get-tuple-element.34.sent_ref), channel_id=1, source_target_pairs={{0,4},{4,0},{1,5},{5,1},{2,6},{6,2},{3,7},{7,3},{8,12},{12,8},{9,1... | collective-permute-start | bytes 811016 | tf_op jit(solution)/shard_map/ppermute | solution.py:306
  5.6 1.1 %shard_map.85 = (f32[256,256]{1,0:T(8,128)S(1)}, f32[256,128]{1,0:T(8,128)S(1)}, f32[256,128]{1,0:T(8,128)S(1)}, f32[256,256]{1,0:T(8,128)S(1)}, f32[256,128]{1,...) custom-call(bf16[256,256]{1,0:T(8,128)(2,1)S(1)} %get-tuple-element.29.q_ref, ...), custom_call_target="tpu_custom_call" | custom-call | flops 100000000 | bytes 2000000 | tf_op jit(solution)/shard_map/pallas_call | solution.py:280
  6.7 0.1 collective-permute-done.got_ref
  6.8 0.1 shard_map.86
  6.9 19.5 %all_to_all.10.msg_ref = f32[288,1,256]{2,1,0:T(1,128)S(1)} all-to-all(f32[288,1,256]{2,1,0:T(1,128)S(1)} %shard_map.86), channel_id=1, replica_groups=mesh['seq_y'=4,'seq_z'=8,'seq_c'=2,'batch'=4] {'seq_y','seq_z'}, dimensions={0} | all-to-all | bytes 589824 | tf_op jit(solution)/shard_map/all_to_all | solution.py:309
  26.4 0.1 shard_map.87
  26.5 16.5 %all_to_all.11 = f32[32,8,256]{2,1,0:T(8,128)S(1)} all-to-all(f32[32,8,256]{2,1,0:T(8,128)S(1)} %bitcast.2), channel_id=1, replica_groups=mesh['seq_y'=4,'seq_z'=8,'seq_c'=2,'batch'=4] {'seq_y','seq_z'}, dimensions={0} | all-to-all | bytes 524288 | tf_op jit(solution)/shard_map/all_to_all | solution.py:311
  43.0 0.1 shard_map.88
  43.1 3.8 %collective-permute-start.1 = (f32[256,256]{1,0:T(8,128)S(1)}, f32[256,256]{1,0:T(8,128)S(1)}, u32[]{:S(2)}, u32[]{:S(2)}) collective-permute-start(f32[256,256]{1,0:T(8,128)S(1)} %get-tuple-element.36), channel_id=1, source_target_pairs={{0,4},{4,0},{1,5},{5,1},{2,6},{6,2},{3,7},{7,3},{8,12},{12,8},{9,1... | collective-permute-start | bytes 786440 | tf_op jit(solution)/shard_map/ppermute | solution.py:315
  46.9 1.2 %shard_map.89 = (bf16[256,128]{1,0:T(8,128)(2,1)S(1)}, bf16[256,128]{1,0:T(8,128)(2,1)S(1)}, bf16[256,256]{1,0:T(8,128)(2,1)S(1)}, f32[256,128]{1,0:T(8,128)S(1)...) custom-call(bf16[256,256]{1,0:T(8,128)(2,1)S(1)} %get-tuple-element., ...), custom_call_target="tpu_custom_call" | custom-call | flops 100000000 | bytes 2000000 | tf_op jit(solution)/shard_map/pallas_call | solution.py:280
  48.1 0.0 collective-permute-done.1.in_ref
  48.1 1.3 %shard_map.90 = (bf16[256,256]{1,0:T(8,128)(2,1)}, bf16[256,256]{1,0:T(8,128)(2,1)}, bf16[256,512]{1,0:T(8,128)(2,1)}, f32[256,256]{1,0:T(8,128)}) custom-call(bf16[256,256]{1,0:T(8,128)(2,1)S(1)} %get-tuple-element.29.q_ref, bf16[256,256]{1,0:T(8,128)(2,1)S(1)} %get-tuple-element.30.k_ref, bf16[256,512]{1,0:T(8,128)(2,1)S(1)} %get-tuple-element.31.v_ref, ...), custom_call_target="tpu_custom_call" | custom-call | flops 1000000 | bytes 2000000 | tf_op jit(solution)/shard_map/pallas_call | solution.py:280
Async XLA Ops:
  2.3 4.5 %collective-permute-start = (f32[264,256]{1,0:T(8,128)S(1)}, f32[264,256]{1,0:T(8,128)S(1)}, u32[]{:S(2)}, u32[]{:S(2)}) collective-permute-start(f32[264,256]{1,0:T(8,128)S(1)} %get-tuple-element.34.sent_ref), channel_id=1, source_target_pairs={{0,4},{4,0},{1,5},{5,1},{2,6},{6,2},{3,7},{7,3},{8,12},{12,8},{9,1... | collective-permute-start | bytes 811016 | tf_op jit(solution)/shard_map/ppermute | solution.py:306
  43.1 5.0 %collective-permute-start.1 = (f32[256,256]{1,0:T(8,128)S(1)}, f32[256,256]{1,0:T(8,128)S(1)}, u32[]{:S(2)}, u32[]{:S(2)}) collective-permute-start(f32[256,256]{1,0:T(8,128)S(1)} %get-tuple-element.36), channel_id=1, source_target_pairs={{0,4},{4,0},{1,5},{5,1},{2,6},{6,2},{3,7},{7,3},{8,12},{12,8},{9,1... | collective-permute-start | bytes 786440 | tf_op jit(solution)/shard_map/ppermute | solution.py:315

commit v4 on v3

--- a/solution.py
+++ b/solution.py
@@ -3,7 +3,6 @@
 from jax import lax
 from jax.experimental import pallas as pl
 from jax.experimental.pallas import tpu as pltpu
-from jax.sharding import Mesh
 from jax.sharding import PartitionSpec as P
 
 H = 2
@@ -17,10 +16,21 @@
 CHIPS = Y * Z
 ROWS = V // CHIPS
 MSG = ROWS + 1
-CHIP_AXES = ("seq_y", "seq_z")
-SPEC = P(("batch", "seq_y", "seq_z", "seq_c"), None)
+SPEC = P(("batch", "seq"), None)
+FIRST = (Y // 2, Z // 2)
+LISTED = [((y + FIRST[0]) % Y) * Z + (z + FIRST[1]) % Z for y in range(Y) for z in range(Z)]
+GROUPS = [[CORES * chip + core for chip in LISTED] for core in range(CORES)]
+SWAP = [(device, device ^ 1) for device in range(CHIPS * CORES)]
 F32 = jnp.float32
 BF16 = jnp.bfloat16
+
+
+def core_index():
+    return lax.rem(lax.axis_index("seq"), CORES)
+
+
+def exchanged(x):
+    return lax.all_to_all(x, "seq", 0, 0, axis_index_groups=GROUPS, tiled=True)
 
 
 def dot(left, right, dims):
@@ -99,7 +109,7 @@
     b_ref[...] = running_sum(g_ref[...])
     for copy in copies[1:]:
         copy.wait()
-    h = 1 - lax.axis_index("seq_c")
+    h = 1 - core_index()
     block_ends(q_ref, k_ref, v_ref, do_ref, b_ref, send_ref, h)
     total = b_ref[TOK - 1 :, at_head(h, K)]
     send_ref[V:] = jnp.broadcast_to(halves(total, total), (8, HK))
@@ -157,14 +167,14 @@
 
 
 def second_kernel(q_ref, k_ref, v_ref, do_ref, b_ref, own_ref, *inner_refs):
-    core = lax.axis_index("seq_c")
+    core = core_index()
     block_ends(q_ref, k_ref, v_ref, do_ref, b_ref, own_ref, core)
     outer_gates(k_ref, b_ref, core, *inner_refs[3:])
     inner_pairs(q_ref, k_ref, v_ref, do_ref, b_ref, core, *inner_refs[:3])
 
 
 def lane_gates(b_ref, got_ref):
-    core = lax.axis_index("seq_c")
+    core = core_index()
     total = b_ref[TOK - 1 :, at_head(core, K)]
     mine = jnp.exp(halves(total, total))
     other = jnp.exp(got_ref[V : V + 1])
@@ -188,7 +198,8 @@
 
 
 def scan_kernel(msg_ref, out_ref):
-    for order, lanes in ((range(CHIPS), slice(0, K)), (range(CHIPS - 1, -1, -1), slice(K, HK))):
+    places = [LISTED.index(chip) for chip in range(CHIPS)]
+    for order, lanes in ((places, slice(0, K)), (places[::-1], slice(K, HK))):
         state = jnp.zeros((ROWS, K), F32)
         for i in order:
             out_ref[i * ROWS : (i + 1) * ROWS, lanes] = state
@@ -235,7 +246,7 @@
 
 
 def own_grads_kernel(q_ref, k_ref, v_ref, do_ref, b_ref, own_ref, in_ref, *rest):
-    core = lax.axis_index("seq_c")
+    core = core_index()
     args = (q_ref, k_ref, v_ref, do_ref, b_ref)
     head_grads(core, *args, own_ref, in_ref, *rest[:6], *rest[6:10], lambda n: None)
     outer_gates(k_ref, b_ref, 1 - core, *rest[13:])
@@ -244,7 +255,7 @@
 
 def final_kernel(q_ref, k_ref, v_ref, do_ref, b_ref, sent_ref, in_ref, *rest):
     inner_refs, mine, outs, theirs, sems = rest[:6], rest[6:10], rest[10:14], rest[14:18], rest[18]
-    core = lax.axis_index("seq_c")
+    core = core_index()
     widths = (K, K, V, K)
 
     def copies(sources, h, base):
@@ -289,9 +300,6 @@
     return out if len(outs) > 1 else out[0]
 
 
-SWAP = [(0, 1), (1, 0)]
-
-
 def local(q, k, v, log_decay, do):
     q, k, v, do, log_decay = (
         pltpu.with_memory_space_constraint(x, pltpu.HBM) for x in (q, k, v, do, log_decay)
@@ -303,16 +311,14 @@
         specs=[HBM] * 5,
         scratch=[pltpu.VMEM((TOK, HK), F32), pltpu.SemaphoreType.DMA((5,))],
     )
-    got = lax.ppermute(send, "seq_c", SWAP)
+    got = lax.ppermute(send, "seq", SWAP)
     own, *inner = call(second_kernel, [SQUARE, *INNER], q, k, v, do, b, flops=100000000)
     msg = call(message_kernel, [((CHIPS * MSG, 1, HK), F32)], own, got, b)
-    msg = lax.all_to_all(msg, CHIP_AXES, 0, 0, tiled=True)
+    msg = exchanged(msg)
     back = call(scan_kernel, [SQUARE], msg)
-    came = lax.all_to_all(
-        back.reshape(CHIPS, ROWS, HK), CHIP_AXES, 0, 0, tiled=True
-    ).reshape(V, HK)
+    came = exchanged(back.reshape(CHIPS, ROWS, HK)).reshape(V, HK)
     onward, mine = call(onward_kernel, [SQUARE, SQUARE], own, got, b, came)
-    theirs = lax.ppermute(onward, "seq_c", SWAP)
+    theirs = lax.ppermute(onward, "seq", SWAP)
     done = call(
         own_grads_kernel,
         HALF_GRADS + INNER,
@@ -329,10 +335,6 @@
 
 
 def solution(mesh):
-    finer = Mesh(
-        mesh.devices.reshape(Y, Z, CORES, mesh.shape["batch"]),
-        ("seq_y", "seq_z", "seq_c", "batch"),
-    )
     return jax.shard_map(
-        local, mesh=finer, in_specs=(SPEC,) * 5, out_specs=(SPEC,) * 4, check_vma=False
-    )
+        local, mesh=mesh, in_specs=(SPEC,) * 5, out_specs=(SPEC,) * 4, check_vma=False
+    )

time: 49.5 us -> 45.7 us (0.923)
  blocking collectives: 36 us -> 33.8 us
  starting transfers between devices: 7.04 us -> 5.41 us
    all_to_all x2, blocking collectives: 36 us -> 33.8 us  [exchanged(): return lax.all_to_all(x, 'seq', 0, 0, axis_index_groups=GROUPS, tiled=True)]
    ppermute x2, starting transfers between devices: 7.04 us -> 5.41 us  [the longest x1 3.29 us: local(): got = lax.ppermute(send, 'seq', SWAP)]
where the time goes in v4:
time: 45.7 us; the launch traced here: 45.5 us
  blocking collectives  33.8 us (74%)
  Pallas kernels  5.52 us (12%)
  starting transfers between devices  5.41 us (12%)
  between operations  0.68 us (1%)
    all_to_all x2, blocking collectives, exchanged(): return lax.all_to_all(x, 'seq', 0, 0, axis_index_groups=GROUPS, tiled=True)  33.8 us
    pallas_call x7, Pallas kernels, call(): pl.pallas_call(kernel, out_shape=shapes, in_specs=specs or [VMEM] * len(a...  5.52 us
    ppermute x1, starting transfers between devices, local(): got = lax.ppermute(send, 'seq', SWAP)  3.29 us
    ppermute x1, starting transfers between devices, local(): theirs = lax.ppermute(onward, 'seq', SWAP)  2.12 us
  transfers between devices with their start and end apart: 2, of which 1 were waited for; matrix products, arithmetic and copies ran while one was open for 0% of the time, Pallas kernels for 5%

profile of v4, /device:TPU:1, one launch (start us, length us, event | category | flops | bytes accessed | tf_op | source)
XLA Modules:
  0.0 45.5 jit_solution(7657538664124130529)
XLA Ops:
  0.6 1.7 %shard_map.84 = (bf16[256,256]{1,0:T(8,128)(2,1)S(1)}, bf16[256,256]{1,0:T(8,128)(2,1)S(1)}, bf16[256,512]{1,0:T(8,128)(2,1)S(1)}, bf16[256,512]{1,0:T(8,128)(2,...) custom-call(bf16[256,256]{1,0:T(8,128)(2,1)} %q_hbm.1, bf16[256,256]{1,0:T(8,128)(2,1)} %k_hbm.1, ...), custom_call_target="tpu_custom_call" | custom-call | flops 1000000 | bytes 2000000 | tf_op jit(solution)/shard_map/pallas_call | solution.py:291
  2.3 3.3 %collective-permute-start = (f32[264,256]{1,0:T(8,128)S(1)}, f32[264,256]{1,0:T(8,128)S(1)}, u32[]{:S(2)}, u32[]{:S(2)}) collective-permute-start(f32[264,256]{1,0:T(8,128)S(1)} %get-tuple-element.34.sent_ref), channel_id=1, source_target_pairs={{0,4},{4,0},{8,12},{12,8},{16,20},{20,16},{24,28},{28,24},{32,36},... | collective-permute-start | bytes 811016 | tf_op jit(solution)/shard_map/ppermute | solution.py:314
  5.6 1.1 %shard_map.85 = (f32[256,256]{1,0:T(8,128)S(1)}, f32[256,128]{1,0:T(8,128)S(1)}, f32[256,128]{1,0:T(8,128)S(1)}, f32[256,256]{1,0:T(8,128)S(1)}, f32[256,128]{1,...) custom-call(bf16[256,256]{1,0:T(8,128)(2,1)S(1)} %get-tuple-element.29.q_ref, ...), custom_call_target="tpu_custom_call" | custom-call | flops 100000000 | bytes 2000000 | tf_op jit(solution)/shard_map/pallas_call | solution.py:291
  6.7 0.1 collective-permute-done.got_ref
  6.8 0.1 shard_map.86
  6.9 18.5 %all_to_all.10.msg_ref = f32[288,1,256]{2,1,0:T(1,128)S(1)} all-to-all(f32[288,1,256]{2,1,0:T(1,128)S(1)} %shard_map.86), channel_id=1, replica_groups={{160,168,176,184,128,136,144,152,224,232,240,248,192,200,208,216,32,40,..., dimensions={0} | all-to-all | bytes 589824 | tf_op jit(solution)/shard_map/all_to_all | solution.py:33
  25.4 0.1 shard_map.87
  25.5 15.3 %all_to_all.11 = f32[32,8,256]{2,1,0:T(8,128)S(1)} all-to-all(f32[32,8,256]{2,1,0:T(8,128)S(1)} %bitcast.2), channel_id=1, replica_groups={{160,168,176,184,128,136,144,152,224,232,240,248,192,200,208,216,32,40,..., dimensions={0} | all-to-all | bytes 524288 | tf_op jit(solution)/shard_map/all_to_all | solution.py:33
  40.8 0.1 shard_map.88
  40.9 2.1 %collective-permute-start.1 = (f32[256,256]{1,0:T(8,128)S(1)}, f32[256,256]{1,0:T(8,128)S(1)}, u32[]{:S(2)}, u32[]{:S(2)}) collective-permute-start(f32[256,256]{1,0:T(8,128)S(1)} %get-tuple-element.36), channel_id=1, source_target_pairs={{0,4},{4,0},{8,12},{12,8},{16,20},{20,16},{24,28},{28,24},{32,36},... | collective-permute-start | bytes 786440 | tf_op jit(solution)/shard_map/ppermute | solution.py:321
  43.0 1.2 %shard_map.89 = (bf16[256,128]{1,0:T(8,128)(2,1)S(1)}, bf16[256,128]{1,0:T(8,128)(2,1)S(1)}, bf16[256,256]{1,0:T(8,128)(2,1)S(1)}, f32[256,128]{1,0:T(8,128)S(1)...) custom-call(bf16[256,256]{1,0:T(8,128)(2,1)S(1)} %get-tuple-element., ...), custom_call_target="tpu_custom_call" | custom-call | flops 100000000 | bytes 2000000 | tf_op jit(solution)/shard_map/pallas_call | solution.py:291
  44.2 0.0 collective-permute-done.1.in_ref
  44.2 1.3 %shard_map.90 = (bf16[256,256]{1,0:T(8,128)(2,1)}, bf16[256,256]{1,0:T(8,128)(2,1)}, bf16[256,512]{1,0:T(8,128)(2,1)}, f32[256,256]{1,0:T(8,128)}) custom-call(bf16[256,256]{1,0:T(8,128)(2,1)S(1)} %get-tuple-element.29.q_ref, bf16[256,256]{1,0:T(8,128)(2,1)S(1)} %get-tuple-element.30.k_ref, bf16[256,512]{1,0:T(8,128)(2,1)S(1)} %get-tuple-element.31.v_ref, ...), custom_call_target="tpu_custom_call" | custom-call | flops 1000000 | bytes 2000000 | tf_op jit(solution)/shard_map/pallas_call | solution.py:291
Async XLA Ops:
  2.3 4.5 %collective-permute-start = (f32[264,256]{1,0:T(8,128)S(1)}, f32[264,256]{1,0:T(8,128)S(1)}, u32[]{:S(2)}, u32[]{:S(2)}) collective-permute-start(f32[264,256]{1,0:T(8,128)S(1)} %get-tuple-element.34.sent_ref), channel_id=1, source_target_pairs={{0,4},{4,0},{8,12},{12,8},{16,20},{20,16},{24,28},{28,24},{32,36},... | collective-permute-start | bytes 811016 | tf_op jit(solution)/shard_map/ppermute | solution.py:314
  40.9 3.3 %collective-permute-start.1 = (f32[256,256]{1,0:T(8,128)S(1)}, f32[256,256]{1,0:T(8,128)S(1)}, u32[]{:S(2)}, u32[]{:S(2)}) collective-permute-start(f32[256,256]{1,0:T(8,128)S(1)} %get-tuple-element.36), channel_id=1, source_target_pairs={{0,4},{4,0},{8,12},{12,8},{16,20},{20,16},{24,28},{28,24},{32,36},... | collective-permute-start | bytes 786440 | tf_op jit(solution)/shard_map/ppermute | solution.py:321

commit v5 on v4

--- a/solution.py
+++ b/solution.py
@@ -15,11 +15,19 @@
 Y, Z, CORES = 4, 8, 2
 CHIPS = Y * Z
 ROWS = V // CHIPS
-MSG = ROWS + 1
+MSG = 2 * ROWS + 1
 SPEC = P(("batch", "seq"), None)
 FIRST = (Y // 2, Z // 2)
-LISTED = [((y + FIRST[0]) % Y) * Z + (z + FIRST[1]) % Z for y in range(Y) for z in range(Z)]
+
+
+def steps(chip):
+    y, z = (chip // Z - FIRST[0]) % Y, (chip % Z - FIRST[1]) % Z
+    return min(y, Y - y) + min(z, Z - z)
+
+
+LISTED = sorted(range(CHIPS), key=steps)
 GROUPS = [[CORES * chip + core for chip in LISTED] for core in range(CORES)]
+LAG_NS = 900
 SWAP = [(device, device ^ 1) for device in range(CHIPS * CORES)]
 F32 = jnp.float32
 BF16 = jnp.bfloat16
@@ -69,9 +77,8 @@
     c = lax.broadcasted_iota(jnp.int32, (rows, rows), 1)
     ones = jnp.where(c <= r, 1.0, 0.0).astype(BF16)
     hi = x.astype(BF16)
-    rest = x - hi.astype(F32)
-    mid, lo = split(rest)
-    return nn(ones, hi) + (nn(ones, mid) + nn(ones, lo))
+    mid, lo = split(x - hi.astype(F32))
+    return folded(nn(ones, halves(hi, mid))) + nn(ones, lo)
 
 
 def head(h, width):
@@ -88,31 +95,38 @@
 
 def block_ends(q_ref, k_ref, v_ref, do_ref, b_ref, out_ref, h):
     hk, hv = at_head(h, K), at_head(h, V)
-    b = b_ref[:, hk]
-    total = b_ref[TOK - 1 :, hk]
+    b = b_ref[...]
+    total = b_ref[TOK - 1 :]
     out_ref[:V, :K] = folded(tn(v_ref[:, hv], pair(k_ref[:, hk].astype(F32) * jnp.exp(total - b))))
     out_ref[:V, K:] = folded(tn(do_ref[:, hv], pair(q_ref[:, hk].astype(F32) * jnp.exp(b))))
 
 
 def first_kernel(
-    q_hbm, k_hbm, v_hbm, do_hbm, g_hbm, q_ref, k_ref, v_ref, do_ref, b_ref, send_ref, g_ref, sems
+    q_hbm, k_hbm, v_hbm, do_hbm, g_hbm, q_ref, k_ref, v_ref, do_ref, g_ref, b_ref, send_ref, sems
 ):
-    copies = [
-        pltpu.make_async_copy(source, target, sems.at[n])
-        for n, (source, target) in enumerate(
-            ((g_hbm, g_ref), (k_hbm, k_ref), (v_hbm, v_ref), (q_hbm, q_ref), (do_hbm, do_ref))
-        )
-    ]
-    for copy in copies:
+    core = core_index()
+    pieces = ((g_hbm, g_ref, K), (k_hbm, k_ref, K), (v_hbm, v_ref, V), (q_hbm, q_ref, K), (do_hbm, do_ref, V))
+
+    def copies(h, base):
+        return [
+            pltpu.make_async_copy(
+                source.at[:, at_head(h, width)], target.at[:, at_head(h, width)], sems.at[base + n]
+            )
+            for n, (source, target, width) in enumerate(pieces)
+        ]
+
+    sent, kept = copies(1 - core, 0), copies(core, len(pieces))
+    for copy in sent + kept:
         copy.start()
-    copies[0].wait()
-    b_ref[...] = running_sum(g_ref[...])
-    for copy in copies[1:]:
+    sent[0].wait()
+    b_ref[...] = running_sum(g_ref[:, at_head(1 - core, K)])
+    for copy in sent[1:]:
         copy.wait()
-    h = 1 - core_index()
-    block_ends(q_ref, k_ref, v_ref, do_ref, b_ref, send_ref, h)
-    total = b_ref[TOK - 1 :, at_head(h, K)]
+    block_ends(q_ref, k_ref, v_ref, do_ref, b_ref, send_ref, 1 - core)
+    total = b_ref[TOK - 1 :]
     send_ref[V:] = jnp.broadcast_to(halves(total, total), (8, HK))
+    for copy in kept:
+        copy.wait()
 
 
 def inner_pairs(q_ref, k_ref, v_ref, do_ref, b_ref, h, dq_ref, dk_ref, dv_ref):
@@ -121,7 +135,7 @@
     c = lax.broadcasted_iota(jnp.int32, (TOK, TOK), 1)
     q = q_ref[:, hk].astype(F32)
     k = k_ref[:, hk].astype(F32)
-    b = b_ref[:, hk]
+    b = b_ref[...]
     v = v_ref[:, hv]
     do = do_ref[:, hv]
     p_hi, p_lo = split(jnp.where(c <= r, nt(do, v), 0.0))
@@ -158,16 +172,16 @@
 
 
 def outer_gates(k_ref, b_ref, h, rise_ref, tail_ref, kt_ref):
-    hk = at_head(h, K)
-    b = b_ref[:, hk]
-    tail = jnp.exp(b_ref[TOK - 1 :, hk] - b)
+    b = b_ref[...]
+    tail = jnp.exp(b_ref[TOK - 1 :] - b)
     rise_ref[...] = jnp.exp(b)
     tail_ref[...] = tail
-    kt_ref[...] = pair(k_ref[:, hk].astype(F32) * tail)
-
-
-def second_kernel(q_ref, k_ref, v_ref, do_ref, b_ref, own_ref, *inner_refs):
-    core = core_index()
+    kt_ref[...] = pair(k_ref[:, at_head(h, K)].astype(F32) * tail)
+
+
+def second_kernel(q_ref, k_ref, v_ref, do_ref, g_ref, b_ref, own_ref, *inner_refs):
+    core = core_index()
+    b_ref[...] = running_sum(g_ref[:, at_head(core, K)])
     block_ends(q_ref, k_ref, v_ref, do_ref, b_ref, own_ref, core)
     outer_gates(k_ref, b_ref, core, *inner_refs[3:])
     inner_pairs(q_ref, k_ref, v_ref, do_ref, b_ref, core, *inner_refs[:3])
@@ -175,7 +189,7 @@
 
 def lane_gates(b_ref, got_ref):
     core = core_index()
-    total = b_ref[TOK - 1 :, at_head(core, K)]
+    total = b_ref[TOK - 1 :]
     mine = jnp.exp(halves(total, total))
     other = jnp.exp(got_ref[V : V + 1])
     forward = lax.broadcasted_iota(jnp.int32, (1, HK), 1) < K
@@ -187,24 +201,30 @@
 
 
 def message_kernel(own_ref, got_ref, b_ref, msg_ref):
+    @pl.when(core_index() == 0)
+    def _():
+        pl.delay(LAG_NS)
+
     mine, other, forward, first = lane_gates(b_ref, got_ref)
     own_gate = pick(first, forward, other, 1.0)
     got_gate = pick(first, forward, 1.0, mine)
-    both = mine * other
     for i in range(CHIPS):
         rows = slice(i * ROWS, (i + 1) * ROWS)
-        msg_ref[i * MSG : i * MSG + ROWS, 0, :] = own_ref[rows] * own_gate + got_ref[rows] * got_gate
-        msg_ref[i * MSG + ROWS] = both
+        chip = own_ref[rows] * own_gate + got_ref[rows] * got_gate
+        for side in range(2):
+            at = i * MSG + side * ROWS
+            msg_ref[at : at + ROWS, 0, :] = chip[:, head(side, K)]
+        msg_ref[i * MSG + 2 * ROWS] = (mine * other)[:, :K]
 
 
 def scan_kernel(msg_ref, out_ref):
     places = [LISTED.index(chip) for chip in range(CHIPS)]
-    for order, lanes in ((places, slice(0, K)), (places[::-1], slice(K, HK))):
+    for side, order in enumerate((places, places[::-1])):
         state = jnp.zeros((ROWS, K), F32)
         for i in order:
-            out_ref[i * ROWS : (i + 1) * ROWS, lanes] = state
-            gate = msg_ref[i * MSG + ROWS, :, lanes]
-            state = gate * state + msg_ref[i * MSG : i * MSG + ROWS, 0, lanes]
+            out_ref[i * ROWS : (i + 1) * ROWS, head(side, K)] = state
+            at = i * MSG + side * ROWS
+            state = msg_ref[i * MSG + 2 * ROWS] * state + msg_ref[at : at + ROWS, 0, :]
 
 
 def onward_kernel(own_ref, got_ref, b_ref, came_ref, send_ref, mine_ref):
@@ -235,7 +255,7 @@
     dv = dvi_ref[...] + (nt(kt_ref[...], halves(g_hi, g_hi)) + nt(kt_ref[:, :K], g_lo))
     dv_ref[...] = dv.astype(BF16)
     stored(2)
-    end_state = jnp.exp(b_ref[TOK - 1 :, hk]) * state + end_ref[:V, :K]
+    end_state = jnp.exp(b_ref[TOK - 1 :]) * state + end_ref[:V, :K]
     later = jnp.sum(end_state * grad, axis=0, keepdims=True)
     terms = q_ref[:, hk].astype(F32) * dq - k_ref[:, hk].astype(F32) * dk
     r = lax.broadcasted_iota(jnp.int32, (TOK, TOK), 0)
@@ -245,12 +265,12 @@
     stored(3)
 
 
-def own_grads_kernel(q_ref, k_ref, v_ref, do_ref, b_ref, own_ref, in_ref, *rest):
-    core = core_index()
-    args = (q_ref, k_ref, v_ref, do_ref, b_ref)
-    head_grads(core, *args, own_ref, in_ref, *rest[:6], *rest[6:10], lambda n: None)
-    outer_gates(k_ref, b_ref, 1 - core, *rest[13:])
-    inner_pairs(*args, 1 - core, *rest[10:13])
+def own_grads_kernel(q_ref, k_ref, v_ref, do_ref, b_ref, b_sent_ref, own_ref, in_ref, *rest):
+    core = core_index()
+    args = (q_ref, k_ref, v_ref, do_ref)
+    head_grads(core, *args, b_ref, own_ref, in_ref, *rest[:6], *rest[6:10], lambda n: None)
+    outer_gates(k_ref, b_sent_ref, 1 - core, *rest[13:])
+    inner_pairs(*args, b_sent_ref, 1 - core, *rest[10:13])
 
 
 def final_kernel(q_ref, k_ref, v_ref, do_ref, b_ref, sent_ref, in_ref, *rest):
@@ -304,16 +324,18 @@
     q, k, v, do, log_decay = (
         pltpu.with_memory_space_constraint(x, pltpu.HBM) for x in (q, k, v, do, log_decay)
     )
-    q, k, v, do, b, send = call(
+    q, k, v, do, log_decay, b_sent, send = call(
         first_kernel,
-        [SQUARE16, SQUARE16, WIDE16, WIDE16, SQUARE, ((V + 8, HK), F32)],
+        [SQUARE16, SQUARE16, WIDE16, WIDE16, SQUARE, HALF, ((V + 8, HK), F32)],
         q, k, v, do, log_decay,
         specs=[HBM] * 5,
-        scratch=[pltpu.VMEM((TOK, HK), F32), pltpu.SemaphoreType.DMA((5,))],
+        scratch=[pltpu.SemaphoreType.DMA((10,))],
     )
     got = lax.ppermute(send, "seq", SWAP)
-    own, *inner = call(second_kernel, [SQUARE, *INNER], q, k, v, do, b, flops=100000000)
-    msg = call(message_kernel, [((CHIPS * MSG, 1, HK), F32)], own, got, b)
+    b, own, *inner = call(
+        second_kernel, [HALF, SQUARE, *INNER], q, k, v, do, log_decay, flops=100000000
+    )
+    msg = call(message_kernel, [((CHIPS * MSG, 1, K), F32)], own, got, b)
     msg = exchanged(msg)
     back = call(scan_kernel, [SQUARE], msg)
     came = exchanged(back.reshape(CHIPS, ROWS, HK)).reshape(V, HK)
@@ -322,13 +344,13 @@
     done = call(
         own_grads_kernel,
         HALF_GRADS + INNER,
-        q, k, v, do, b, own, mine, *inner,
+        q, k, v, do, b, b_sent, own, mine, *inner,
         flops=100000000,
     )
     return call(
         final_kernel,
         [SQUARE16, SQUARE16, WIDE16, SQUARE],
-        q, k, v, do, b, send, theirs, *done[4:], *done[:4],
+        q, k, v, do, b_sent, send, theirs, *done[4:], *done[:4],
         out_specs=[HBM] * 4,
         scratch=[pltpu.VMEM(*out) for out in HALF_GRADS] + [pltpu.SemaphoreType.DMA((8,))],
     )

time: 45.7 us -> 44.3 us (0.969)
  blocking collectives: 33.8 us -> 31.2 us
  starting transfers between devices: 5.41 us -> 6.63 us
    all_to_all x2, blocking collectives: 33.8 us -> 31.2 us  [exchanged(): return lax.all_to_all(x, 'seq', 0, 0, axis_index_groups=GROUPS, tiled=True)]
    ppermute x1, starting transfers between devices: 2.12 us -> 3.34 us  [local(): theirs = lax.ppermute(onward, 'seq', SWAP)]
  transfers between devices with their start and end apart: 2 -> 2, of which waited for: 1 -> 0; matrix products, arithmetic and copies ran while one was open for 0% -> 0% of each run, Pallas kernels for 5% -> 6%
where the time goes in v5:
time: 44.3 us; the launch traced here: 44.2 us
  blocking collectives  31.2 us (70%)
  starting transfers between devices  6.63 us (15%)
  Pallas kernels  5.66 us (13%)
  between operations  0.68 us (2%)
    all_to_all x2, blocking collectives, exchanged(): return lax.all_to_all(x, 'seq', 0, 0, axis_index_groups=GROUPS, tiled=True)  31.2 us
    pallas_call x7, Pallas kernels, call(): pl.pallas_call(kernel, out_shape=shapes, in_specs=specs or [VMEM] * len(a...  5.66 us
    ppermute x1, starting transfers between devices, local(): theirs = lax.ppermute(onward, 'seq', SWAP)  3.34 us
    ppermute x1, starting transfers between devices, local(): got = lax.ppermute(send, 'seq', SWAP)  3.29 us
  transfers between devices with their start and end apart: 2, of which 0 were waited for; matrix products, arithmetic and copies ran while one was open for 0% of the time, Pallas kernels for 6%

profile of v5, /device:TPU:1, one launch (start us, length us, event | category | flops | bytes accessed | tf_op | source)
XLA Modules:
  0.0 44.2 jit_solution(17624915821253688836)
XLA Ops:
  0.6 1.5 %shard_map.84 = (bf16[256,256]{1,0:T(8,128)(2,1)S(1)}, bf16[256,256]{1,0:T(8,128)(2,1)S(1)}, bf16[256,512]{1,0:T(8,128)(2,1)S(1)}, bf16[256,512]{1,0:T(8,128)(2,...) custom-call(bf16[256,256]{1,0:T(8,128)(2,1)} %q_hbm.1, bf16[256,256]{1,0:T(8,128)(2,1)} %k_hbm.1, ...), custom_call_target="tpu_custom_call" | custom-call | flops 1000000 | bytes 2000000 | tf_op jit(solution)/shard_map/pallas_call | solution.py:311
  2.2 3.3 %collective-permute-start = (f32[264,256]{1,0:T(8,128)S(1)}, f32[264,256]{1,0:T(8,128)S(1)}, u32[]{:S(2)}, u32[]{:S(2)}) collective-permute-start(f32[264,256]{1,0:T(8,128)S(1)} %get-tuple-element.36.sent_ref), channel_id=1, source_target_pairs={{0,4},{4,0},{8,12},{12,8},{16,20},{20,16},{24,28},{28,24},{32,36},... | collective-permute-start | bytes 811016 | tf_op jit(solution)/shard_map/ppermute | solution.py:334
  5.5 1.3 %shard_map.85 = (f32[256,128]{1,0:T(8,128)S(1)}, f32[256,256]{1,0:T(8,128)S(1)}, f32[256,128]{1,0:T(8,128)S(1)}, f32[256,128]{1,0:T(8,128)S(1)}, f32[256,256]{1,...) custom-call(bf16[256,256]{1,0:T(8,128)(2,1)S(1)} %get-tuple-element.31.q_ref, ...), custom_call_target="tpu_custom_call" | custom-call | flops 100000000 | bytes 2000000 | tf_op jit(solution)/shard_map/pallas_call | solution.py:311
  6.8 0.0 collective-permute-done.got_ref
  6.8 0.2 shard_map.86
  7.0 17.7 %all_to_all.10.msg_ref = f32[544,1,128]{2,1,0:T(1,128)S(1)} all-to-all(f32[544,1,128]{2,1,0:T(1,128)S(1)} %shard_map.86), channel_id=1, replica_groups={{160,96,152,168,224,32,88,104,144,176,216,232,24,40,80,112,136,184,208,..., dimensions={0} | all-to-all | bytes 557056 | tf_op jit(solution)/shard_map/all_to_all | solution.py:41
  24.6 0.1 shard_map.87
  24.8 13.5 %all_to_all.11 = f32[32,8,256]{2,1,0:T(8,128)S(1)} all-to-all(f32[32,8,256]{2,1,0:T(8,128)S(1)} %bitcast.3), channel_id=1, replica_groups={{160,96,152,168,224,32,88,104,144,176,216,232,24,40,80,112,136,184,208,..., dimensions={0} | all-to-all | bytes 524288 | tf_op jit(solution)/shard_map/all_to_all | solution.py:41
  38.3 0.1 shard_map.88
  38.4 3.3 %collective-permute-start.1 = (f32[256,256]{1,0:T(8,128)S(1)}, f32[256,256]{1,0:T(8,128)S(1)}, u32[]{:S(2)}, u32[]{:S(2)}) collective-permute-start(f32[256,256]{1,0:T(8,128)S(1)} %get-tuple-element.40), channel_id=1, source_target_pairs={{0,4},{4,0},{8,12},{12,8},{16,20},{20,16},{24,28},{28,24},{32,36},... | collective-permute-start | bytes 786440 | tf_op jit(solution)/shard_map/ppermute | solution.py:343
  41.7 1.2 %shard_map.89 = (bf16[256,128]{1,0:T(8,128)(2,1)S(1)}, bf16[256,128]{1,0:T(8,128)(2,1)S(1)}, bf16[256,256]{1,0:T(8,128)(2,1)S(1)}, f32[256,128]{1,0:T(8,128)S(1)...) custom-call(bf16[256,256]{1,0:T(8,128)(2,1)S(1)} %get-tuple-element., ...), custom_call_target="tpu_custom_call" | custom-call | flops 100000000 | bytes 2000000 | tf_op jit(solution)/shard_map/pallas_call | solution.py:311
  42.9 0.0 collective-permute-done.1.in_ref
  42.9 1.3 %shard_map.90 = (bf16[256,256]{1,0:T(8,128)(2,1)}, bf16[256,256]{1,0:T(8,128)(2,1)}, bf16[256,512]{1,0:T(8,128)(2,1)}, f32[256,256]{1,0:T(8,128)}) custom-call(bf16[256,256]{1,0:T(8,128)(2,1)S(1)} %get-tuple-element.31.q_ref, bf16[256,256]{1,0:T(8,128)(2,1)S(1)} %get-tuple-element.32.k_ref, bf16[256,512]{1,0:T(8,128)(2,1)S(1)} %get-tuple-element.33.v_ref, ...), custom_call_target="tpu_custom_call" | custom-call | flops 1000000 | bytes 2000000 | tf_op jit(solution)/shard_map/pallas_call | solution.py:311
Async XLA Ops:
  2.2 4.6 %collective-permute-start = (f32[264,256]{1,0:T(8,128)S(1)}, f32[264,256]{1,0:T(8,128)S(1)}, u32[]{:S(2)}, u32[]{:S(2)}) collective-permute-start(f32[264,256]{1,0:T(8,128)S(1)} %get-tuple-element.36.sent_ref), channel_id=1, source_target_pairs={{0,4},{4,0},{8,12},{12,8},{16,20},{20,16},{24,28},{28,24},{32,36},... | collective-permute-start | bytes 811016 | tf_op jit(solution)/shard_map/ppermute | solution.py:334
  38.4 4.5 %collective-permute-start.1 = (f32[256,256]{1,0:T(8,128)S(1)}, f32[256,256]{1,0:T(8,128)S(1)}, u32[]{:S(2)}, u32[]{:S(2)}) collective-permute-start(f32[256,256]{1,0:T(8,128)S(1)} %get-tuple-element.40), channel_id=1, source_target_pairs={{0,4},{4,0},{8,12},{12,8},{16,20},{20,16},{24,28},{28,24},{32,36},... | collective-permute-start | bytes 786440 | tf_op jit(solution)/shard_map/ppermute | solution.py:343

commit v6 on v5

--- a/solution.py
+++ b/solution.py
@@ -27,7 +27,6 @@
 
 LISTED = sorted(range(CHIPS), key=steps)
 GROUPS = [[CORES * chip + core for chip in LISTED] for core in range(CORES)]
-LAG_NS = 900
 SWAP = [(device, device ^ 1) for device in range(CHIPS * CORES)]
 F32 = jnp.float32
 BF16 = jnp.bfloat16
@@ -179,12 +178,20 @@
     kt_ref[...] = pair(k_ref[:, at_head(h, K)].astype(F32) * tail)
 
 
-def second_kernel(q_ref, k_ref, v_ref, do_ref, g_ref, b_ref, own_ref, *inner_refs):
+def both_inner(q_ref, k_ref, v_ref, do_ref, b_ref, b_sent_ref, core, inner_refs):
+    for h, sums_ref, refs in ((core, b_ref, inner_refs[:6]), (1 - core, b_sent_ref, inner_refs[6:])):
+        inner_pairs(q_ref, k_ref, v_ref, do_ref, sums_ref, h, *refs[:3])
+        outer_gates(k_ref, sums_ref, h, *refs[3:])
+
+
+def second_kernel(q_ref, k_ref, v_ref, do_ref, g_ref, b_sent_ref, b_ref, own_ref, *inner_refs):
     core = core_index()
     b_ref[...] = running_sum(g_ref[:, at_head(core, K)])
     block_ends(q_ref, k_ref, v_ref, do_ref, b_ref, own_ref, core)
-    outer_gates(k_ref, b_ref, core, *inner_refs[3:])
-    inner_pairs(q_ref, k_ref, v_ref, do_ref, b_ref, core, *inner_refs[:3])
+
+    @pl.when(core == 0)
+    def _():
+        both_inner(q_ref, k_ref, v_ref, do_ref, b_ref, b_sent_ref, core, inner_refs)
 
 
 def lane_gates(b_ref, got_ref):
@@ -201,10 +208,6 @@
 
 
 def message_kernel(own_ref, got_ref, b_ref, msg_ref):
-    @pl.when(core_index() == 0)
-    def _():
-        pl.delay(LAG_NS)
-
     mine, other, forward, first = lane_gates(b_ref, got_ref)
     own_gate = pick(first, forward, other, 1.0)
     got_gate = pick(first, forward, 1.0, mine)
@@ -227,7 +230,11 @@
             state = msg_ref[i * MSG + 2 * ROWS] * state + msg_ref[at : at + ROWS, 0, :]
 
 
-def onward_kernel(own_ref, got_ref, b_ref, came_ref, send_ref, mine_ref):
+def onward_kernel(
+    own_ref, got_ref, b_ref, came_ref, q_ref, k_ref, v_ref, do_ref, b_sent_ref, *rest
+):
+    send_ref, mine_ref = rest[12:14]
+    core = core_index()
     mine, other, forward, first = lane_gates(b_ref, got_ref)
     came = came_ref[...]
     send_ref[...] = came * pick(first, forward, mine, 1.0) + pick(
@@ -236,6 +243,10 @@
     mine_ref[...] = came * pick(first, forward, 1.0, other) + pick(
         first, forward, 0.0, got_ref[:V]
     )
+
+    @pl.when(core == 1)
+    def _():
+        both_inner(q_ref, k_ref, v_ref, do_ref, b_ref, b_sent_ref, core, rest[14:])
 
 
 def head_grads(
@@ -265,12 +276,10 @@
     stored(3)
 
 
-def own_grads_kernel(q_ref, k_ref, v_ref, do_ref, b_ref, b_sent_ref, own_ref, in_ref, *rest):
-    core = core_index()
-    args = (q_ref, k_ref, v_ref, do_ref)
-    head_grads(core, *args, b_ref, own_ref, in_ref, *rest[:6], *rest[6:10], lambda n: None)
-    outer_gates(k_ref, b_sent_ref, 1 - core, *rest[13:])
-    inner_pairs(*args, b_sent_ref, 1 - core, *rest[10:13])
+def own_grads_kernel(q_ref, k_ref, v_ref, do_ref, b_ref, own_ref, in_ref, *rest):
+    head_grads(
+        core_index(), q_ref, k_ref, v_ref, do_ref, b_ref, own_ref, in_ref, *rest, lambda n: None
+    )
 
 
 def final_kernel(q_ref, k_ref, v_ref, do_ref, b_ref, sent_ref, in_ref, *rest):
@@ -306,7 +315,7 @@
 HALF_GRADS = [((TOK, K), BF16), ((TOK, K), BF16), ((TOK, V), BF16), HALF]
 
 
-def call(kernel, outs, *args, specs=None, out_specs=None, scratch=(), flops=1000000):
+def call(kernel, outs, *args, specs=None, out_specs=None, scratch=(), flops=1000000, alias=None):
     shapes = [jax.ShapeDtypeStruct(shape, dtype) for shape, dtype in outs]
     out = pl.pallas_call(
         kernel,
@@ -314,6 +323,7 @@
         in_specs=specs or [VMEM] * len(args),
         out_specs=out_specs or [VMEM] * len(outs),
         scratch_shapes=list(scratch),
+        input_output_aliases=alias or {},
         cost_estimate=pl.CostEstimate(flops=flops, bytes_accessed=2000000, transcendentals=0),
         compiler_params=pltpu.CompilerParams(vmem_limit_bytes=32 << 20),
     )(*args)
@@ -333,24 +343,27 @@
     )
     got = lax.ppermute(send, "seq", SWAP)
     b, own, *inner = call(
-        second_kernel, [HALF, SQUARE, *INNER], q, k, v, do, log_decay, flops=100000000
+        second_kernel, [HALF, SQUARE, *INNER, *INNER], q, k, v, do, log_decay, b_sent,
+        flops=100000000,
     )
     msg = call(message_kernel, [((CHIPS * MSG, 1, K), F32)], own, got, b)
     msg = exchanged(msg)
     back = call(scan_kernel, [SQUARE], msg)
     came = exchanged(back.reshape(CHIPS, ROWS, HK)).reshape(V, HK)
-    onward, mine = call(onward_kernel, [SQUARE, SQUARE], own, got, b, came)
+    onward, mine, *inner = call(
+        onward_kernel,
+        [SQUARE, SQUARE, *INNER, *INNER],
+        own, got, b, came, q, k, v, do, b_sent, *inner,
+        alias={9 + n: 2 + n for n in range(12)},
+    )
     theirs = lax.ppermute(onward, "seq", SWAP)
     done = call(
-        own_grads_kernel,
-        HALF_GRADS + INNER,
-        q, k, v, do, b, b_sent, own, mine, *inner,
-        flops=100000000,
+        own_grads_kernel, HALF_GRADS, q, k, v, do, b, own, mine, *inner[:6], flops=100000000
     )
     return call(
         final_kernel,
         [SQUARE16, SQUARE16, WIDE16, SQUARE],
-        q, k, v, do, b_sent, send, theirs, *done[4:], *done[:4],
+        q, k, v, do, b_sent, send, theirs, *inner[6:], *done,
         out_specs=[HBM] * 4,
         scratch=[pltpu.VMEM(*out) for out in HALF_GRADS] + [pltpu.SemaphoreType.DMA((8,))],
     )

time: 44.3 us -> 44.2 us (level)
  starting transfers between devices: 6.63 us -> 4.91 us
  waiting for transfers between devices: 0.01 us -> 1.36 us
    ppermute x1, starting transfers between devices: 3.34 us -> 1.62 us  [local(): theirs = lax.ppermute(onward, 'seq', SWAP)]
    ppermute x1, waiting for transfers between devices: 0.01 us -> 0.68 us  [local(): theirs = lax.ppermute(onward, 'seq', SWAP)]
    ppermute x1, waiting for transfers between devices: 0.01 us -> 0.68 us  [local(): got = lax.ppermute(send, 'seq', SWAP)]
  transfers between devices with their start and end apart: 2 -> 2, of which waited for: 0 -> 2; matrix products, arithmetic and copies ran while one was open for 0% -> 0% of each run, Pallas kernels for 6% -> 2%
where the time goes in v6:
time: 44.2 us; the launch traced here: 44 us
  blocking collectives  31.2 us (71%)
  Pallas kernels  5.88 us (13%)
  starting transfers between devices  4.91 us (11%)
  waiting for transfers between devices  1.36 us (3%)
  between operations  0.67 us (2%)
    all_to_all x2, blocking collectives, exchanged(): return lax.all_to_all(x, 'seq', 0, 0, axis_index_groups=GROUPS, tiled=True)  31.2 us
    pallas_call x7, Pallas kernels, call(): pl.pallas_call(kernel, out_shape=shapes, in_specs=specs or [VMEM] * len(a...  5.88 us
    ppermute x1, starting transfers between devices, local(): got = lax.ppermute(send, 'seq', SWAP)  3.29 us
    ppermute x1, starting transfers between devices, local(): theirs = lax.ppermute(onward, 'seq', SWAP)  1.62 us
  transfers between devices with their start and end apart: 2, of which 2 were waited for; matrix products, arithmetic and copies ran while one was open for 0% of the time, Pallas kernels for 2%

profile of v6, /device:TPU:1, one launch (start us, length us, event | category | flops | bytes accessed | tf_op | source)
XLA Modules:
  0.0 44.0 jit_solution(13582102473011754978)
XLA Ops:
  0.6 1.5 %shard_map.84 = (bf16[256,256]{1,0:T(8,128)(2,1)S(1)}, bf16[256,256]{1,0:T(8,128)(2,1)S(1)}, bf16[256,512]{1,0:T(8,128)(2,1)S(1)}, bf16[256,512]{1,0:T(8,128)(2,...) custom-call(bf16[256,256]{1,0:T(8,128)(2,1)} %q_hbm.1, bf16[256,256]{1,0:T(8,128)(2,1)} %k_hbm.1, ...), custom_call_target="tpu_custom_call" | custom-call | flops 1000000 | bytes 2000000 | tf_op jit(solution)/shard_map/pallas_call | solution.py:320
  2.2 3.3 %collective-permute-start = (f32[264,256]{1,0:T(8,128)S(1)}, f32[264,256]{1,0:T(8,128)S(1)}, u32[]{:S(2)}, u32[]{:S(2)}) collective-permute-start(f32[264,256]{1,0:T(8,128)S(1)} %get-tuple-element.48.sent_ref), channel_id=1, source_target_pairs={{0,4},{4,0},{8,12},{12,8},{16,20},{20,16},{24,28},{28,24},{32,36},... | collective-permute-start | bytes 811016 | tf_op jit(solution)/shard_map/ppermute | solution.py:344
  5.5 0.5 %shard_map.85 = (f32[256,128]{1,0:T(8,128)S(1)}, f32[256,256]{1,0:T(8,128)S(1)}, f32[256,128]{1,0:T(8,128)S(1)}, f32[256,128]{1,0:T(8,128)S(1)}, f32[256,256]{1,...) custom-call(bf16[256,256]{1,0:T(8,128)(2,1)S(1)} %get-tuple-element., ...), custom_call_target="tpu_custom_call" | custom-call | flops 100000000 | bytes 2000000 | tf_op jit(solution)/shard_map/pallas_call | solution.py:320
  6.0 0.7 %collective-permute-done.got_ref = f32[264,256]{1,0:T(8,128)S(1)} collective-permute-done((f32[264,256]{1,0:T(8,128)S(1)}, f32[264,256]{1,0:T(8,128)S(1)}, u32[]{:S(2)}, u32[]{:S(2)}) %collective-permute-start) | collective-permute-done | bytes 270368 | tf_op jit(solution)/shard_map/ppermute | solution.py:344
  6.6 0.2 shard_map.86
  6.8 17.6 %all_to_all.10.msg_ref = f32[544,1,128]{2,1,0:T(1,128)S(1)} all-to-all(f32[544,1,128]{2,1,0:T(1,128)S(1)} %shard_map.86), channel_id=1, replica_groups={{160,96,152,168,224,32,88,104,144,176,216,232,24,40,80,112,136,184,208,..., dimensions={0} | all-to-all | bytes 557056 | tf_op jit(solution)/shard_map/all_to_all | solution.py:40
  24.5 0.1 shard_map.87
  24.6 13.5 %all_to_all.11 = f32[32,8,256]{2,1,0:T(8,128)S(1)} all-to-all(f32[32,8,256]{2,1,0:T(8,128)S(1)} %bitcast.3), channel_id=1, replica_groups={{160,96,152,168,224,32,88,104,144,176,216,232,24,40,80,112,136,184,208,..., dimensions={0} | all-to-all | bytes 524288 | tf_op jit(solution)/shard_map/all_to_all | solution.py:40
  38.1 1.8 %shard_map.88 = (f32[256,256]{1,0:T(8,128)S(1)}, f32[256,256]{1,0:T(8,128)S(1)}, f32[256,128]{1,0:T(8,128)S(1)}, f32[256,128]{1,0:T(8,128)S(1)}, f32[256,256]{1,...) custom-call(f32[256,256]{1,0:T(8,128)S(1)} %get-tuple-element.50.own, ...), custom_call_target="tpu_custom_call", output_to_operand_aliasing={{2}: (9, {}), {3}: (10, {}), {4}: (11, {}), {5}: (12, {}), ... | custom-call | flops 1000000 | bytes 2000000 | tf_op jit(solution)/shard_map/pallas_call | solution.py:320
  39.9 1.6 %collective-permute-start.1 = (f32[256,256]{1,0:T(8,128)S(1)}, f32[256,256]{1,0:T(8,128)S(1)}, u32[]{:S(2)}, u32[]{:S(2)}) collective-permute-start(f32[256,256]{1,0:T(8,128)S(1)} %get-tuple-element.64), channel_id=1, source_target_pairs={{0,4},{4,0},{8,12},{12,8},{16,20},{20,16},{24,28},{28,24},{32,36},... | collective-permute-start | bytes 786440 | tf_op jit(solution)/shard_map/ppermute | solution.py:359
  41.6 0.5 %shard_map.89 = (bf16[256,128]{1,0:T(8,128)(2,1)S(1)}, bf16[256,128]{1,0:T(8,128)(2,1)S(1)}, bf16[256,256]{1,0:T(8,128)(2,1)S(1)}, f32[256,128]{1,0:T(8,128)S(1)}) custom-call(bf16[256,256]{1,0:T(8,128)(2,1)S(1)} %get-tuple-element.43.q_ref, bf16[256,256]{1,0:T(8,128)(2,1)S(1)} %get-tuple-element.44.k_ref, bf16[256,512]{1,0:T(8,128)(2,1)S(1)} %get-tuple-element.45.v_ref, ...), custom_call_target="tpu_custom_call" | custom-call | flops 100000000 | bytes 2000000 | tf_op jit(solution)/shard_map/pallas_call | solution.py:320
  42.0 0.7 %collective-permute-done.1.in_ref = f32[256,256]{1,0:T(8,128)S(1)} collective-permute-done((f32[256,256]{1,0:T(8,128)S(1)}, f32[256,256]{1,0:T(8,128)S(1)}, u32[]{:S(2)}, u32[]{:S(2)}) %collective-permute-start.1) | collective-permute-done | bytes 262176 | tf_op jit(solution)/shard_map/ppermute | solution.py:359
  42.7 1.3 %shard_map.90 = (bf16[256,256]{1,0:T(8,128)(2,1)}, bf16[256,256]{1,0:T(8,128)(2,1)}, bf16[256,512]{1,0:T(8,128)(2,1)}, f32[256,256]{1,0:T(8,128)}) custom-call(bf16[256,256]{1,0:T(8,128)(2,1)S(1)} %get-tuple-element.43.q_ref, bf16[256,256]{1,0:T(8,128)(2,1)S(1)} %get-tuple-element.44.k_ref, bf16[256,512]{1,0:T(8,128)(2,1)S(1)} %get-tuple-element.45.v_ref, ...), custom_call_target="tpu_custom_call" | custom-call | flops 1000000 | bytes 2000000 | tf_op jit(solution)/shard_map/pallas_call | solution.py:320
Async XLA Ops:
  2.2 4.5 %collective-permute-start = (f32[264,256]{1,0:T(8,128)S(1)}, f32[264,256]{1,0:T(8,128)S(1)}, u32[]{:S(2)}, u32[]{:S(2)}) collective-permute-start(f32[264,256]{1,0:T(8,128)S(1)} %get-tuple-element.48.sent_ref), channel_id=1, source_target_pairs={{0,4},{4,0},{8,12},{12,8},{16,20},{20,16},{24,28},{28,24},{32,36},... | collective-permute-start | bytes 811016 | tf_op jit(solution)/shard_map/ppermute | solution.py:344
  39.9 2.8 %collective-permute-start.1 = (f32[256,256]{1,0:T(8,128)S(1)}, f32[256,256]{1,0:T(8,128)S(1)}, u32[]{:S(2)}, u32[]{:S(2)}) collective-permute-start(f32[256,256]{1,0:T(8,128)S(1)} %get-tuple-element.64), channel_id=1, source_target_pairs={{0,4},{4,0},{8,12},{12,8},{16,20},{20,16},{24,28},{28,24},{32,36},... | collective-permute-start | bytes 786440 | tf_op jit(solution)/shard_map/ppermute | solution.py:359

commit v7 on v6

--- a/solution.py
+++ b/solution.py
@@ -276,32 +276,19 @@
     stored(3)
 
 
-def own_grads_kernel(q_ref, k_ref, v_ref, do_ref, b_ref, own_ref, in_ref, *rest):
+def grads_kernel(own, q_ref, k_ref, v_ref, do_ref, b_ref, end_ref, in_ref, *rest):
+    inner_refs, outs, halves_out, sems = rest[:6], rest[-9:-5], rest[-5:-1], rest[-1]
+    core = core_index()
+    h = core if own else 1 - core
+    copies = [
+        pltpu.make_async_copy(source, out.at[:, at_head(h, width)], sems.at[n])
+        for n, (source, out, width) in enumerate(zip(halves_out, outs, (K, K, V, K)))
+    ]
     head_grads(
-        core_index(), q_ref, k_ref, v_ref, do_ref, b_ref, own_ref, in_ref, *rest, lambda n: None
-    )
-
-
-def final_kernel(q_ref, k_ref, v_ref, do_ref, b_ref, sent_ref, in_ref, *rest):
-    inner_refs, mine, outs, theirs, sems = rest[:6], rest[6:10], rest[10:14], rest[14:18], rest[18]
-    core = core_index()
-    widths = (K, K, V, K)
-
-    def copies(sources, h, base):
-        return [
-            pltpu.make_async_copy(source, out.at[:, at_head(h, width)], sems.at[base + n])
-            for n, (source, out, width) in enumerate(zip(sources, outs, widths))
-        ]
-
-    first = copies(mine, core, 0)
-    second = copies(theirs, 1 - core, 4)
-    for copy in first:
-        copy.start()
-    head_grads(
-        1 - core, q_ref, k_ref, v_ref, do_ref, b_ref, sent_ref, in_ref, *inner_refs, *theirs,
-        lambda n: second[n].start(),
-    )
-    for copy in first + second:
+        h, q_ref, k_ref, v_ref, do_ref, b_ref, end_ref, in_ref, *inner_refs, *halves_out,
+        lambda n: copies[n].start(),
+    )
+    for copy in copies:
         copy.wait()
 
 
@@ -330,6 +317,23 @@
     return out if len(outs) > 1 else out[0]
 
 
+def grads(own, args, into=()):
+    def kernel(*refs):
+        grads_kernel(own, *refs)
+
+    return call(
+        kernel,
+        [SQUARE16, SQUARE16, WIDE16, SQUARE],
+        *args,
+        *into,
+        specs=[VMEM] * len(args) + [HBM] * len(into),
+        out_specs=[HBM] * 4,
+        scratch=[pltpu.VMEM(*out) for out in HALF_GRADS] + [pltpu.SemaphoreType.DMA((4,))],
+        flops=100000000,
+        alias={len(args) + n: n for n in range(len(into))},
+    )
+
+
 def local(q, k, v, log_decay, do):
     q, k, v, do, log_decay = (
         pltpu.with_memory_space_constraint(x, pltpu.HBM) for x in (q, k, v, do, log_decay)
@@ -357,16 +361,8 @@
         alias={9 + n: 2 + n for n in range(12)},
     )
     theirs = lax.ppermute(onward, "seq", SWAP)
-    done = call(
-        own_grads_kernel, HALF_GRADS, q, k, v, do, b, own, mine, *inner[:6], flops=100000000
-    )
-    return call(
-        final_kernel,
-        [SQUARE16, SQUARE16, WIDE16, SQUARE],
-        q, k, v, do, b_sent, send, theirs, *inner[6:], *done,
-        out_specs=[HBM] * 4,
-        scratch=[pltpu.VMEM(*out) for out in HALF_GRADS] + [pltpu.SemaphoreType.DMA((8,))],
-    )
+    half = grads(True, (q, k, v, do, b, own, mine, *inner[:6]))
+    return grads(False, (q, k, v, do, b_sent, send, theirs, *inner[6:]), half)
 
 
 def solution(mesh):

time: 44.2 us -> 44.1 us (level)
  waiting for transfers between devices: 1.36 us -> 0.68 us
  Pallas kernels: 5.88 us -> 6.46 us
    ppermute x1, waiting for transfers between devices: 0.68 us -> 0.01 us  [local(): theirs = lax.ppermute(onward, 'seq', SWAP)]
    pallas_call x7, Pallas kernels: 5.88 us -> 6.46 us  [call(): pl.pallas_call(kernel, out_shape=shapes, in_specs=specs or [VMEM] * len(a...]
  transfers between devices with their start and end apart: 2 -> 2, of which waited for: 2 -> 1; matrix products, arithmetic and copies ran while one was open for 0% -> 0% of each run, Pallas kernels for 2% -> 4%
where the time goes in v7:
time: 44.1 us; the launch traced here: 43.9 us
  blocking collectives  31.2 us (71%)
  Pallas kernels  6.46 us (15%)
  starting transfers between devices  4.91 us (11%)
  waiting for transfers between devices  0.68 us (2%)
  between operations  0.68 us (2%)
    all_to_all x2, blocking collectives, exchanged(): return lax.all_to_all(x, 'seq', 0, 0, axis_index_groups=GROUPS, tiled=True)  31.2 us
    pallas_call x7, Pallas kernels, call(): pl.pallas_call(kernel, out_shape=shapes, in_specs=specs or [VMEM] * len(a...  6.46 us
    ppermute x1, starting transfers between devices, local(): got = lax.ppermute(send, 'seq', SWAP)  3.29 us
    ppermute x1, starting transfers between devices, local(): theirs = lax.ppermute(onward, 'seq', SWAP)  1.62 us
  transfers between devices with their start and end apart: 2, of which 1 were waited for; matrix products, arithmetic and copies ran while one was open for 0% of the time, Pallas kernels for 4%

profile of v7, /device:TPU:1, one launch (start us, length us, event | category | flops | bytes accessed | tf_op | source)
XLA Modules:
  0.0 43.9 jit_solution(14935304851745877201)
XLA Ops:
  0.6 1.5 %shard_map.84 = (bf16[256,256]{1,0:T(8,128)(2,1)S(1)}, bf16[256,256]{1,0:T(8,128)(2,1)S(1)}, bf16[256,512]{1,0:T(8,128)(2,1)S(1)}, bf16[256,512]{1,0:T(8,128)(2,...) custom-call(bf16[256,256]{1,0:T(8,128)(2,1)} %q_hbm.1, bf16[256,256]{1,0:T(8,128)(2,1)} %k_hbm.1, ...), custom_call_target="tpu_custom_call" | custom-call | flops 1000000 | bytes 2000000 | tf_op jit(solution)/shard_map/pallas_call | solution.py:307
  2.2 3.3 %collective-permute-start = (f32[264,256]{1,0:T(8,128)S(1)}, f32[264,256]{1,0:T(8,128)S(1)}, u32[]{:S(2)}, u32[]{:S(2)}) collective-permute-start(f32[264,256]{1,0:T(8,128)S(1)} %get-tuple-element.48.refs_5_), channel_id=1, source_target_pairs={{0,4},{4,0},{8,12},{12,8},{16,20},{20,16},{24,28},{28,24},{32,36},... | collective-permute-start | bytes 811016 | tf_op jit(solution)/shard_map/ppermute | solution.py:348
  5.5 0.5 %shard_map.85 = (f32[256,128]{1,0:T(8,128)S(1)}, f32[256,256]{1,0:T(8,128)S(1)}, f32[256,128]{1,0:T(8,128)S(1)}, f32[256,128]{1,0:T(8,128)S(1)}, f32[256,256]{1,...) custom-call(bf16[256,256]{1,0:T(8,128)(2,1)S(1)} %get-tuple-element., ...), custom_call_target="tpu_custom_call" | custom-call | flops 100000000 | bytes 2000000 | tf_op jit(solution)/shard_map/pallas_call | solution.py:307
  6.0 0.7 %collective-permute-done.got_ref = f32[264,256]{1,0:T(8,128)S(1)} collective-permute-done((f32[264,256]{1,0:T(8,128)S(1)}, f32[264,256]{1,0:T(8,128)S(1)}, u32[]{:S(2)}, u32[]{:S(2)}) %collective-permute-start) | collective-permute-done | bytes 270368 | tf_op jit(solution)/shard_map/ppermute | solution.py:348
  6.6 0.2 shard_map.86
  6.8 17.6 %all_to_all.10.msg_ref = f32[544,1,128]{2,1,0:T(1,128)S(1)} all-to-all(f32[544,1,128]{2,1,0:T(1,128)S(1)} %shard_map.86), channel_id=1, replica_groups={{160,96,152,168,224,32,88,104,144,176,216,232,24,40,80,112,136,184,208,..., dimensions={0} | all-to-all | bytes 557056 | tf_op jit(solution)/shard_map/all_to_all | solution.py:40
  24.5 0.1 shard_map.87
  24.6 13.5 %all_to_all.11 = f32[32,8,256]{2,1,0:T(8,128)S(1)} all-to-all(f32[32,8,256]{2,1,0:T(8,128)S(1)} %bitcast.3), channel_id=1, replica_groups={{160,96,152,168,224,32,88,104,144,176,216,232,24,40,80,112,136,184,208,..., dimensions={0} | all-to-all | bytes 524288 | tf_op jit(solution)/shard_map/all_to_all | solution.py:40
  38.1 1.8 %shard_map.88 = (f32[256,256]{1,0:T(8,128)S(1)}, f32[256,256]{1,0:T(8,128)S(1)}, f32[256,128]{1,0:T(8,128)S(1)}, f32[256,128]{1,0:T(8,128)S(1)}, f32[256,256]{1,...) custom-call(f32[256,256]{1,0:T(8,128)S(1)} %get-tuple-element.50.own, ...), custom_call_target="tpu_custom_call", output_to_operand_aliasing={{2}: (9, {}), {3}: (10, {}), {4}: (11, {}), {5}: (12, {}), ... | custom-call | flops 1000000 | bytes 2000000 | tf_op jit(solution)/shard_map/pallas_call | solution.py:307
  39.9 1.6 %collective-permute-start.1 = (f32[256,256]{1,0:T(8,128)S(1)}, f32[256,256]{1,0:T(8,128)S(1)}, u32[]{:S(2)}, u32[]{:S(2)}) collective-permute-start(f32[256,256]{1,0:T(8,128)S(1)} %get-tuple-element.64), channel_id=1, source_target_pairs={{0,4},{4,0},{8,12},{12,8},{16,20},{20,16},{24,28},{28,24},{32,36},... | collective-permute-start | bytes 786440 | tf_op jit(solution)/shard_map/ppermute | solution.py:363
  41.6 1.2 %shard_map.89 = (bf16[256,256]{1,0:T(8,128)(2,1)}, bf16[256,256]{1,0:T(8,128)(2,1)}, bf16[256,512]{1,0:T(8,128)(2,1)}, f32[256,256]{1,0:T(8,128)}) custom-call(bf16[256,256]{1,0:T(8,128)(2,1)S(1)} %get-tuple-element.43.q_ref.refs_0_, bf16[256,256]{1,0:T(8,128)(2,1)S(1)} %get-tuple-element.44.k_ref.refs_1_, ...), custom_call_target="tpu_custom_call" | custom-call | flops 100000000 | bytes 2000000 | tf_op jit(solution)/shard_map/pallas_call | solution.py:307
  42.7 0.0 collective-permute-done.1.refs_6_
  42.7 1.2 %shard_map.90 = (bf16[256,256]{1,0:T(8,128)(2,1)}, bf16[256,256]{1,0:T(8,128)(2,1)}, bf16[256,512]{1,0:T(8,128)(2,1)}, f32[256,256]{1,0:T(8,128)}) custom-call(bf16[256,256]{1,0:T(8,128)(2,1)S(1)} %get-tuple-element.43.q_ref.refs_0_, ...), custom_call_target="tpu_custom_call", output_to_operand_aliasing={{0}: (13, {}), {1}: (14, {}), {2}: (15, {}), {3}: (16, {})} | custom-call | flops 100000000 | bytes 2000000 | tf_op jit(solution)/shard_map/pallas_call | solution.py:307
Async XLA Ops:
  2.2 4.5 %collective-permute-start = (f32[264,256]{1,0:T(8,128)S(1)}, f32[264,256]{1,0:T(8,128)S(1)}, u32[]{:S(2)}, u32[]{:S(2)}) collective-permute-start(f32[264,256]{1,0:T(8,128)S(1)} %get-tuple-element.48.refs_5_), channel_id=1, source_target_pairs={{0,4},{4,0},{8,12},{12,8},{16,20},{20,16},{24,28},{28,24},{32,36},... | collective-permute-start | bytes 811016 | tf_op jit(solution)/shard_map/ppermute | solution.py:348
  39.9 2.8 %collective-permute-start.1 = (f32[256,256]{1,0:T(8,128)S(1)}, f32[256,256]{1,0:T(8,128)S(1)}, u32[]{:S(2)}, u32[]{:S(2)}) collective-permute-start(f32[256,256]{1,0:T(8,128)S(1)} %get-tuple-element.64), channel_id=1, source_target_pairs={{0,4},{4,0},{8,12},{12,8},{16,20},{20,16},{24,28},{28,24},{32,36},... | collective-permute-start | bytes 786440 | tf_op jit(solution)/shard_map/ppermute | solution.py:363

commit v8 on v7

--- a/solution.py
+++ b/solution.py
@@ -25,7 +25,12 @@
     return min(y, Y - y) + min(z, Z - z)
 
 
-LISTED = sorted(range(CHIPS), key=steps)
+def steps_along_z(chip):
+    z = (chip % Z - FIRST[1]) % Z
+    return min(z, Z - z)
+
+
+LISTED = sorted(range(CHIPS), key=lambda chip: (steps_along_z(chip), steps(chip)))
 GROUPS = [[CORES * chip + core for chip in LISTED] for core in range(CORES)]
 SWAP = [(device, device ^ 1) for device in range(CHIPS * CORES)]
 F32 = jnp.float32
@@ -257,15 +262,15 @@
     state = in_ref[:, :K]
     grad = in_ref[:, K:]
     g_hi, g_lo = split(grad)
+    dv = dvi_ref[...] + (nt(kt_ref[...], halves(g_hi, g_hi)) + nt(kt_ref[:, :K], g_lo))
+    dv_ref[...] = dv.astype(BF16)
+    stored(2)
     dq = dqi_ref[...] + rise_ref[...] * folded(nn(do_ref[:, hv], pair(state)))
     dk = dki_ref[...] + tail_ref[...] * folded(nn(v_ref[:, hv], halves(g_hi, g_lo)))
     dq_ref[...] = dq.astype(BF16)
     stored(0)
     dk_ref[...] = dk.astype(BF16)
     stored(1)
-    dv = dvi_ref[...] + (nt(kt_ref[...], halves(g_hi, g_hi)) + nt(kt_ref[:, :K], g_lo))
-    dv_ref[...] = dv.astype(BF16)
-    stored(2)
     end_state = jnp.exp(b_ref[TOK - 1 :]) * state + end_ref[:V, :K]
     later = jnp.sum(end_state * grad, axis=0, keepdims=True)
     terms = q_ref[:, hk].astype(F32) * dq - k_ref[:, hk].astype(F32) * dk

time: 44.1 us -> 44.1 us (level)
  no operation moved by 1% of the time
where the time goes in v8:
time: 44.1 us; the launch traced here: 43.9 us
  blocking collectives  31.3 us (71%)
  Pallas kernels  6.46 us (15%)
  starting transfers between devices  4.81 us (11%)
  waiting for transfers between devices  0.68 us (2%)
  between operations  0.68 us (2%)
    all_to_all x2, blocking collectives, exchanged(): return lax.all_to_all(x, 'seq', 0, 0, axis_index_groups=GROUPS, tiled=True)  31.3 us
    pallas_call x7, Pallas kernels, call(): pl.pallas_call(kernel, out_shape=shapes, in_specs=specs or [VMEM] * len(a...  6.46 us
    ppermute x1, starting transfers between devices, local(): got = lax.ppermute(send, 'seq', SWAP)  3.29 us
    ppermute x1, starting transfers between devices, local(): theirs = lax.ppermute(onward, 'seq', SWAP)  1.52 us
  transfers between devices with their start and end apart: 2, of which 1 were waited for; matrix products, arithmetic and copies ran while one was open for 0% of the time, Pallas kernels for 4%

profile of v8, /device:TPU:1, one launch (start us, length us, event | category | flops | bytes accessed | tf_op | source)
XLA Modules:
  0.0 43.9 jit_solution(1888660679246464032)
XLA Ops:
  0.6 1.5 %shard_map.84 = (bf16[256,256]{1,0:T(8,128)(2,1)S(1)}, bf16[256,256]{1,0:T(8,128)(2,1)S(1)}, bf16[256,512]{1,0:T(8,128)(2,1)S(1)}, bf16[256,512]{1,0:T(8,128)(2,...) custom-call(bf16[256,256]{1,0:T(8,128)(2,1)} %q_hbm.1, bf16[256,256]{1,0:T(8,128)(2,1)} %k_hbm.1, ...), custom_call_target="tpu_custom_call" | custom-call | flops 1000000 | bytes 2000000 | tf_op jit(solution)/shard_map/pallas_call | solution.py:312
  2.2 3.3 %collective-permute-start = (f32[264,256]{1,0:T(8,128)S(1)}, f32[264,256]{1,0:T(8,128)S(1)}, u32[]{:S(2)}, u32[]{:S(2)}) collective-permute-start(f32[264,256]{1,0:T(8,128)S(1)} %get-tuple-element.48.refs_5_), channel_id=1, source_target_pairs={{0,4},{4,0},{8,12},{12,8},{16,20},{20,16},{24,28},{28,24},{32,36},... | collective-permute-start | bytes 811016 | tf_op jit(solution)/shard_map/ppermute | solution.py:353
  5.5 0.5 %shard_map.85 = (f32[256,128]{1,0:T(8,128)S(1)}, f32[256,256]{1,0:T(8,128)S(1)}, f32[256,128]{1,0:T(8,128)S(1)}, f32[256,128]{1,0:T(8,128)S(1)}, f32[256,256]{1,...) custom-call(bf16[256,256]{1,0:T(8,128)(2,1)S(1)} %get-tuple-element., ...), custom_call_target="tpu_custom_call" | custom-call | flops 100000000 | bytes 2000000 | tf_op jit(solution)/shard_map/pallas_call | solution.py:312
  6.0 0.7 %collective-permute-done.got_ref = f32[264,256]{1,0:T(8,128)S(1)} collective-permute-done((f32[264,256]{1,0:T(8,128)S(1)}, f32[264,256]{1,0:T(8,128)S(1)}, u32[]{:S(2)}, u32[]{:S(2)}) %collective-permute-start) | collective-permute-done | bytes 270368 | tf_op jit(solution)/shard_map/ppermute | solution.py:353
  6.6 0.2 shard_map.86
  6.8 17.6 %all_to_all.10.msg_ref = f32[544,1,128]{2,1,0:T(1,128)S(1)} all-to-all(f32[544,1,128]{2,1,0:T(1,128)S(1)} %shard_map.86), channel_id=1, replica_groups={{160,96,224,32,152,168,88,104,216,232,24,40,144,176,80,112,208,240,16,4..., dimensions={0} | all-to-all | bytes 557056 | tf_op jit(solution)/shard_map/all_to_all | solution.py:45
  24.5 0.1 shard_map.87
  24.6 13.7 %all_to_all.11 = f32[32,8,256]{2,1,0:T(8,128)S(1)} all-to-all(f32[32,8,256]{2,1,0:T(8,128)S(1)} %bitcast.3), channel_id=1, replica_groups={{160,96,224,32,152,168,88,104,216,232,24,40,144,176,80,112,208,240,16,4..., dimensions={0} | all-to-all | bytes 524288 | tf_op jit(solution)/shard_map/all_to_all | solution.py:45
  38.3 1.8 %shard_map.88 = (f32[256,256]{1,0:T(8,128)S(1)}, f32[256,256]{1,0:T(8,128)S(1)}, f32[256,128]{1,0:T(8,128)S(1)}, f32[256,128]{1,0:T(8,128)S(1)}, f32[256,256]{1,...) custom-call(f32[256,256]{1,0:T(8,128)S(1)} %get-tuple-element.50.own, ...), custom_call_target="tpu_custom_call", output_to_operand_aliasing={{2}: (9, {}), {3}: (10, {}), {4}: (11, {}), {5}: (12, {}), ... | custom-call | flops 1000000 | bytes 2000000 | tf_op jit(solution)/shard_map/pallas_call | solution.py:312
  40.1 1.5 %collective-permute-start.1 = (f32[256,256]{1,0:T(8,128)S(1)}, f32[256,256]{1,0:T(8,128)S(1)}, u32[]{:S(2)}, u32[]{:S(2)}) collective-permute-start(f32[256,256]{1,0:T(8,128)S(1)} %get-tuple-element.64), channel_id=1, source_target_pairs={{0,4},{4,0},{8,12},{12,8},{16,20},{20,16},{24,28},{28,24},{32,36},... | collective-permute-start | bytes 786440 | tf_op jit(solution)/shard_map/ppermute | solution.py:368
  41.6 1.2 %shard_map.89 = (bf16[256,256]{1,0:T(8,128)(2,1)}, bf16[256,256]{1,0:T(8,128)(2,1)}, bf16[256,512]{1,0:T(8,128)(2,1)}, f32[256,256]{1,0:T(8,128)}) custom-call(bf16[256,256]{1,0:T(8,128)(2,1)S(1)} %get-tuple-element.43.q_ref.refs_0_, bf16[256,256]{1,0:T(8,128)(2,1)S(1)} %get-tuple-element.44.k_ref.refs_1_, ...), custom_call_target="tpu_custom_call" | custom-call | flops 100000000 | bytes 2000000 | tf_op jit(solution)/shard_map/pallas_call | solution.py:312
  42.7 0.0 collective-permute-done.1.refs_6_
  42.8 1.2 %shard_map.90 = (bf16[256,256]{1,0:T(8,128)(2,1)}, bf16[256,256]{1,0:T(8,128)(2,1)}, bf16[256,512]{1,0:T(8,128)(2,1)}, f32[256,256]{1,0:T(8,128)}) custom-call(bf16[256,256]{1,0:T(8,128)(2,1)S(1)} %get-tuple-element.43.q_ref.refs_0_, ...), custom_call_target="tpu_custom_call", output_to_operand_aliasing={{0}: (13, {}), {1}: (14, {}), {2}: (15, {}), {3}: (16, {})} | custom-call | flops 100000000 | bytes 2000000 | tf_op jit(solution)/shard_map/pallas_call | solution.py:312
Async XLA Ops:
  2.2 4.5 %collective-permute-start = (f32[264,256]{1,0:T(8,128)S(1)}, f32[264,256]{1,0:T(8,128)S(1)}, u32[]{:S(2)}, u32[]{:S(2)}) collective-permute-start(f32[264,256]{1,0:T(8,128)S(1)} %get-tuple-element.48.refs_5_), channel_id=1, source_target_pairs={{0,4},{4,0},{8,12},{12,8},{16,20},{20,16},{24,28},{28,24},{32,36},... | collective-permute-start | bytes 811016 | tf_op jit(solution)/shard_map/ppermute | solution.py:353
  40.1 2.7 %collective-permute-start.1 = (f32[256,256]{1,0:T(8,128)S(1)}, f32[256,256]{1,0:T(8,128)S(1)}, u32[]{:S(2)}, u32[]{:S(2)}) collective-permute-start(f32[256,256]{1,0:T(8,128)S(1)} %get-tuple-element.64), channel_id=1, source_target_pairs={{0,4},{4,0},{8,12},{12,8},{16,20},{20,16},{24,28},{28,24},{32,36},... | collective-permute-start | bytes 786440 | tf_op jit(solution)/shard_map/ppermute | solution.py:368

commit v9 on v7

--- a/solution.py
+++ b/solution.py
@@ -115,8 +115,10 @@
         ]
 
     sent, kept = copies(1 - core, 0), copies(core, len(pieces))
-    for copy in sent + kept:
+    for copy in sent:
         copy.start()
+    for copy in kept:
+        copy.start(priority=1)
     sent[0].wait()
     b_ref[...] = running_sum(g_ref[:, at_head(1 - core, K)])
     for copy in sent[1:]:

time: 44.1 us -> 44.1 us (level)
  no operation moved by 1% of the time
where the time goes in v9:
time: 44.1 us; the launch traced here: 43.9 us
  blocking collectives  31.2 us (71%)
  Pallas kernels  6.46 us (15%)
  starting transfers between devices  4.91 us (11%)
  waiting for transfers between devices  0.68 us (2%)
  between operations  0.68 us (2%)
    all_to_all x2, blocking collectives, exchanged(): return lax.all_to_all(x, 'seq', 0, 0, axis_index_groups=GROUPS, tiled=True)  31.2 us
    pallas_call x7, Pallas kernels, call(): pl.pallas_call(kernel, out_shape=shapes, in_specs=specs or [VMEM] * len(a...  6.46 us
    ppermute x1, starting transfers between devices, local(): got = lax.ppermute(send, 'seq', SWAP)  3.29 us
    ppermute x1, starting transfers between devices, local(): theirs = lax.ppermute(onward, 'seq', SWAP)  1.62 us
  transfers between devices with their start and end apart: 2, of which 1 were waited for; matrix products, arithmetic and copies ran while one was open for 0% of the time, Pallas kernels for 4%

profile of v9, /device:TPU:1, one launch (start us, length us, event | category | flops | bytes accessed | tf_op | source)
XLA Modules:
  0.0 43.9 jit_solution(15571494309130690983)
XLA Ops:
  0.6 1.5 %shard_map.84 = (bf16[256,256]{1,0:T(8,128)(2,1)S(1)}, bf16[256,256]{1,0:T(8,128)(2,1)S(1)}, bf16[256,512]{1,0:T(8,128)(2,1)S(1)}, bf16[256,512]{1,0:T(8,128)(2,...) custom-call(bf16[256,256]{1,0:T(8,128)(2,1)} %q_hbm.1, bf16[256,256]{1,0:T(8,128)(2,1)} %k_hbm.1, ...), custom_call_target="tpu_custom_call" | custom-call | flops 1000000 | bytes 2000000 | tf_op jit(solution)/shard_map/pallas_call | solution.py:309
  2.2 3.3 %collective-permute-start = (f32[264,256]{1,0:T(8,128)S(1)}, f32[264,256]{1,0:T(8,128)S(1)}, u32[]{:S(2)}, u32[]{:S(2)}) collective-permute-start(f32[264,256]{1,0:T(8,128)S(1)} %get-tuple-element.48.refs_5_), channel_id=1, source_target_pairs={{0,4},{4,0},{8,12},{12,8},{16,20},{20,16},{24,28},{28,24},{32,36},... | collective-permute-start | bytes 811016 | tf_op jit(solution)/shard_map/ppermute | solution.py:350
  5.5 0.5 %shard_map.85 = (f32[256,128]{1,0:T(8,128)S(1)}, f32[256,256]{1,0:T(8,128)S(1)}, f32[256,128]{1,0:T(8,128)S(1)}, f32[256,128]{1,0:T(8,128)S(1)}, f32[256,256]{1,...) custom-call(bf16[256,256]{1,0:T(8,128)(2,1)S(1)} %get-tuple-element., ...), custom_call_target="tpu_custom_call" | custom-call | flops 100000000 | bytes 2000000 | tf_op jit(solution)/shard_map/pallas_call | solution.py:309
  6.0 0.7 %collective-permute-done.got_ref = f32[264,256]{1,0:T(8,128)S(1)} collective-permute-done((f32[264,256]{1,0:T(8,128)S(1)}, f32[264,256]{1,0:T(8,128)S(1)}, u32[]{:S(2)}, u32[]{:S(2)}) %collective-permute-start) | collective-permute-done | bytes 270368 | tf_op jit(solution)/shard_map/ppermute | solution.py:350
  6.6 0.2 shard_map.86
  6.8 17.6 %all_to_all.10.msg_ref = f32[544,1,128]{2,1,0:T(1,128)S(1)} all-to-all(f32[544,1,128]{2,1,0:T(1,128)S(1)} %shard_map.86), channel_id=1, replica_groups={{160,96,152,168,224,32,88,104,144,176,216,232,24,40,80,112,136,184,208,..., dimensions={0} | all-to-all | bytes 557056 | tf_op jit(solution)/shard_map/all_to_all | solution.py:40
  24.5 0.1 shard_map.87
  24.6 13.5 %all_to_all.11 = f32[32,8,256]{2,1,0:T(8,128)S(1)} all-to-all(f32[32,8,256]{2,1,0:T(8,128)S(1)} %bitcast.3), channel_id=1, replica_groups={{160,96,152,168,224,32,88,104,144,176,216,232,24,40,80,112,136,184,208,..., dimensions={0} | all-to-all | bytes 524288 | tf_op jit(solution)/shard_map/all_to_all | solution.py:40
  38.1 1.8 %shard_map.88 = (f32[256,256]{1,0:T(8,128)S(1)}, f32[256,256]{1,0:T(8,128)S(1)}, f32[256,128]{1,0:T(8,128)S(1)}, f32[256,128]{1,0:T(8,128)S(1)}, f32[256,256]{1,...) custom-call(f32[256,256]{1,0:T(8,128)S(1)} %get-tuple-element.50.own, ...), custom_call_target="tpu_custom_call", output_to_operand_aliasing={{2}: (9, {}), {3}: (10, {}), {4}: (11, {}), {5}: (12, {}), ... | custom-call | flops 1000000 | bytes 2000000 | tf_op jit(solution)/shard_map/pallas_call | solution.py:309
  39.9 1.6 %collective-permute-start.1 = (f32[256,256]{1,0:T(8,128)S(1)}, f32[256,256]{1,0:T(8,128)S(1)}, u32[]{:S(2)}, u32[]{:S(2)}) collective-permute-start(f32[256,256]{1,0:T(8,128)S(1)} %get-tuple-element.64), channel_id=1, source_target_pairs={{0,4},{4,0},{8,12},{12,8},{16,20},{20,16},{24,28},{28,24},{32,36},... | collective-permute-start | bytes 786440 | tf_op jit(solution)/shard_map/ppermute | solution.py:365
  41.6 1.2 %shard_map.89 = (bf16[256,256]{1,0:T(8,128)(2,1)}, bf16[256,256]{1,0:T(8,128)(2,1)}, bf16[256,512]{1,0:T(8,128)(2,1)}, f32[256,256]{1,0:T(8,128)}) custom-call(bf16[256,256]{1,0:T(8,128)(2,1)S(1)} %get-tuple-element.43.q_ref.refs_0_, bf16[256,256]{1,0:T(8,128)(2,1)S(1)} %get-tuple-element.44.k_ref.refs_1_, ...), custom_call_target="tpu_custom_call" | custom-call | flops 100000000 | bytes 2000000 | tf_op jit(solution)/shard_map/pallas_call | solution.py:309
  42.7 0.0 collective-permute-done.1.refs_6_
  42.7 1.2 %shard_map.90 = (bf16[256,256]{1,0:T(8,128)(2,1)}, bf16[256,256]{1,0:T(8,128)(2,1)}, bf16[256,512]{1,0:T(8,128)(2,1)}, f32[256,256]{1,0:T(8,128)}) custom-call(bf16[256,256]{1,0:T(8,128)(2,1)S(1)} %get-tuple-element.43.q_ref.refs_0_, ...), custom_call_target="tpu_custom_call", output_to_operand_aliasing={{0}: (13, {}), {1}: (14, {}), {2}: (15, {}), {3}: (16, {})} | custom-call | flops 100000000 | bytes 2000000 | tf_op jit(solution)/shard_map/pallas_call | solution.py:309
Async XLA Ops:
  2.2 4.5 %collective-permute-start = (f32[264,256]{1,0:T(8,128)S(1)}, f32[264,256]{1,0:T(8,128)S(1)}, u32[]{:S(2)}, u32[]{:S(2)}) collective-permute-start(f32[264,256]{1,0:T(8,128)S(1)} %get-tuple-element.48.refs_5_), channel_id=1, source_target_pairs={{0,4},{4,0},{8,12},{12,8},{16,20},{20,16},{24,28},{28,24},{32,36},... | collective-permute-start | bytes 811016 | tf_op jit(solution)/shard_map/ppermute | solution.py:350
  39.9 2.8 %collective-permute-start.1 = (f32[256,256]{1,0:T(8,128)S(1)}, f32[256,256]{1,0:T(8,128)S(1)}, u32[]{:S(2)}, u32[]{:S(2)}) collective-permute-start(f32[256,256]{1,0:T(8,128)S(1)} %get-tuple-element.64), channel_id=1, source_target_pairs={{0,4},{4,0},{8,12},{12,8},{16,20},{20,16},{24,28},{28,24},{32,36},... | collective-permute-start | bytes 786440 | tf_op jit(solution)/shard_map/ppermute | solution.py:365
